TPU v7x, 16 devices: a whole 2x2x2 slice. The times are simulated.
16 devices in a mesh: data: 16 (over z, y, x, core).
Axes of the slice: x: 2, y: 2, z: 2, core: 2. Of those that a mesh axis runs over, the one named last changes fastest.
Arguments:
- grad_attn: bfloat16 [16, 4, 1638400], P('data')
- grad_mlp: bfloat16 [16, 2, 6553600], P('data')
- grad_wide: bfloat16 [16, 1, 5120], P('data')
- grad_vec: bfloat16 [16, 11, 1280], P('data')
- weight_attn: float32 [4, 1638400], P(None, 'data')
- weight_mlp: float32 [2, 6553600], P(None, 'data')
- weight_wide: float32 [1, 5120], P(None, 'data')
- weight_vec: float32 [11, 1280], P(None, 'data')
- mom1_attn: float32 [4, 1638400], P(None, 'data')
- mom1_mlp: float32 [2, 6553600], P(None, 'data')
- mom1_wide: float32 [1, 5120], P(None, 'data')
- mom1_vec: float32 [11, 1280], P(None, 'data')
- mom2_attn: float32 [4, 1638400], P(None, 'data')
- mom2_mlp: float32 [2, 6553600], P(None, 'data')
- mom2_wide: float32 [1, 5120], P(None, 'data')
- mom2_vec: float32 [11, 1280], P(None, 'data')
Outputs:
- output 1: bfloat16 [4, 1638400], replicated
- output 2: bfloat16 [2, 6553600], replicated
- output 3: bfloat16 [1, 5120], replicated
- output 4: bfloat16 [11, 1280], replicated
- output 5: float32 [4, 1638400], P(None, 'data')
- output 6: float32 [2, 6553600], P(None, 'data')
- output 7: float32 [1, 5120], P(None, 'data')
- output 8: float32 [11, 1280], P(None, 'data')
- output 9: float32 [4, 1638400], P(None, 'data')
- output 10: float32 [2, 6553600], P(None, 'data')
- output 11: float32 [1, 5120], P(None, 'data')
- output 12: float32 [11, 1280], P(None, 'data')
- output 13: float32 [4, 1638400], P(None, 'data')
- output 14: float32 [2, 6553600], P(None, 'data')
- output 15: float32 [1, 5120], P(None, 'data')
- output 16: float32 [11, 1280], P(None, 'data')
All inputs are finite; a program needn't handle non-finite values.
Results may differ from a plain program's by a relative error of at most 0.001.
Values are sent between devices in bfloat16 or wider.
A program may use at most 1 GiB of HBM per device.

v0:
```python
import jax
import jax.numpy as jnp
from jax import lax
from jax.sharding import PartitionSpec as P

STEP_NUMBER = 10
LEARN_RATE = 0.04
BETA_FIRST = 0.9
BETA_SECOND = 0.999
EPSILON = 1e-6
WEIGHT_DECAY = 0.01
MAX_NORM = 1.0


def adam_direction(mean_grad, weight, first_moment, second_moment, clip_coef):
    clipped = clip_coef * mean_grad
    new_first = BETA_FIRST * first_moment + (1.0 - BETA_FIRST) * clipped
    new_second = BETA_SECOND * second_moment + (1.0 - BETA_SECOND) * (clipped * clipped)
    update = (new_first / (1.0 - BETA_FIRST ** STEP_NUMBER)) / (jnp.sqrt(new_second / (1.0 - BETA_SECOND ** STEP_NUMBER)) + EPSILON) + WEIGHT_DECAY * weight
    return update, new_first, new_second


def solution(mesh):
    group_size = mesh.shape["data"]
    grad_spec = P("data", None, None)
    shard_spec = P(None, "data")
    full_spec = P(None, None)

    def local_step(*all_banks):
        grad_banks = all_banks[0:4]
        weights = all_banks[4:8]
        firsts = all_banks[8:12]
        seconds = all_banks[12:16]
        mean_grads = []
        for grad_bank in grad_banks:
            row_count = grad_bank.shape[1]
            shard_width = grad_bank.shape[2] // group_size
            by_owner = grad_bank.reshape(row_count, group_size, shard_width)
            received = lax.all_to_all(by_owner, "data", 1, 1, tiled=True)
            mean_grads.append(jnp.sum(received, axis=1, dtype=jnp.float32) / group_size)
        local_square = sum(jnp.sum(mean_grad * mean_grad) for mean_grad in mean_grads)
        clip_coef = jnp.minimum(1.0, MAX_NORM / jnp.sqrt(lax.psum(local_square, "data")))
        results = [adam_direction(mean_grads[bank_index], weights[bank_index], firsts[bank_index], seconds[bank_index], clip_coef) for bank_index in range(4)]
        part_sums = jnp.concatenate([jnp.sum(weight * weight, axis=1) for weight in weights] + [jnp.sum(result[0] * result[0], axis=1) for result in results])
        norm_sums = lax.psum(part_sums, "data")
        tensor_count = norm_sums.shape[0] // 2
        trust_ratios = jnp.sqrt(norm_sums[:tensor_count]) / jnp.sqrt(norm_sums[tensor_count:])
        replicas, new_weights = [], []
        first_row = 0
        for bank_index in range(4):
            row_count = weights[bank_index].shape[0]
            trust_ratio = trust_ratios[first_row:first_row + row_count]
            first_row = first_row + row_count
            new_weight = weights[bank_index] - LEARN_RATE * trust_ratio[:, None] * results[bank_index][0]
            new_weights.append(new_weight)
            replicas.append(lax.all_gather(new_weight.astype(jnp.bfloat16), "data", axis=1, tiled=True))
        return tuple(replicas + new_weights + [result[1] for result in results] + [result[2] for result in results])

    return jax.shard_map(local_step, mesh=mesh, in_specs=(grad_spec,) * 4 + (shard_spec,) * 12, out_specs=(full_spec,) * 4 + (shard_spec,) * 12, check_vma=False)
```

profile of v0, /device:TPU:0, one launch (start us, length us, event | category | flops | bytes accessed | tf_op | source)
XLA Modules:
  0.0 840.9 jit_solution(17399252642464548760)
XLA Ops:
  7.2 0.8 reduce.4
  8.6 0.7 reduce.7
  9.3 0.7 reshape.105
  10.0 5.3 all-to-all-start.2
  15.3 0.9 reshape.97
  16.3 4.3 all-to-all-done.2
  20.7 6.9 all_to_all.20
  27.6 149.4 %all_to_all.21 = bf16[4,16,102400]{2,0,1:T(4,128)(2,1)} all-to-all(bf16[4,16,102400]{2,0,1:T(4,128)(2,1)} %bitcast.21), channel_id=1, replica_groups=mesh['data'=16] {'data'}, dimensions={1} | all-to-all | bytes 26214400 | tf_op jit(solution)/shard_map/all_to_all | solution.py:39
  177.1 7.7 all-to-all-start.1
  186.3 18.5 %convert_reduce_fusion.1 = f32[4,102400]{1,0:T(4,128)S(1)} fusion(bf16[4,16,102400]{2,0,1:T(4,128)(2,1)} %all_to_all.21), kind=kLoop, calls=%fused_computation.1 | loop fusion | flops 12697600 | bytes 14745600 | tf_op jit(solution)/shard_map/reduce_sum | solution.py:40
  204.9 1.2 copy-done
  206.0 1.4 multiply_reduce_fusion.4
  207.5 291.6 %all-to-all-done.1 = bf16[2,16,409600]{2,0,1:T(2,128)(2,1)} async-done(((bf16[2,16,409600]{2,0,1:T(2,128)(2,1)}), bf16[2,16,409600]{2,0,1:T(2,128)(2,1)}, u32[]{:S(2)}, u32[]{:S(2)}) %all-to-all-start.1) | async-done | bytes 26214432 | tf_op jit(solution)/shard_map/all_to_all | solution.py:39
  499.1 24.8 %convert_reduce_fusion = f32[2,409600]{1,0:T(2,128)S(1)} fusion(bf16[2,16,409600]{2,0,1:T(2,128)(2,1)} %all-to-all-done.1), kind=kLoop, calls=%fused_computation | loop fusion | flops 25395200 | bytes 29491200 | tf_op jit(solution)/shard_map/reduce_sum | solution.py:40
  523.9 4.0 multiply_reduce_fusion.1
  530.5 33.1 %psum.14 = f32[]{:T(128)} all-reduce(f32[]{:T(128)S(6)} %add.75), channel_id=1, replica_groups=mesh['data'=16] {'data'}, use_global_device_ids=true, to_apply=%region_12.0 | all-reduce | flops 1 | bytes 8 | tf_op jit(solution)/shard_map/psum | solution.py:42
  564.3 16.5 %multiply_reduce_fusion = (f32[2]{0:T(128)S(1)}, f32[2,409600]{1,0:T(2,128)}, f32[2,409600]{1,0:T(2,128)}, f32[2,409600]{1,0:T(2,128)}, f32[2]{0:T(128)S(1)}) fusion(f32[2,409600]{1,0:T(2,128)} %param.21, f32[2,409600]{1,0:T(2,128)S(1)} %convert_reduce_fusion, f32[]{:T(128)S(6)} %mul.303, f32[2,409600]{1,0:T(2,128)} %param.25, f32[2,409600]{1,0:T(2,128)} %param.29), kind=kLoop, calls=%fused_computation.3 | loop fusion | flops 14745596 | bytes 22937620 | tf_op jit(solution)/shard_map/reduce_sum | solution.py:44
  581.0 4.7 multiply_reduce_fusion.3
  585.9 1.2 multiply_reduce_fusion.10
  587.1 1.4 concatenate.3
  588.5 32.6 %psum.15 = f32[36]{0:T(128)S(1)} all-reduce(f32[36]{0:T(128)S(1)} %concatenate.3), channel_id=1, replica_groups=mesh['data'=16] {'data'}, use_global_device_ids=true, to_apply=%region_17.0 | all-reduce | flops 36 | bytes 288 | tf_op jit(solution)/shard_map/psum | solution.py:45
  621.3 4.1 fusion.1
  625.5 5.8 fusion
  631.9 0.7 convert_bitcast_fusion
  632.6 14.2 %all-gather = bf16[16,80,11]{1,2,0:T(8,128)(2,1)S(1)} all-gather(bf16[1,80,11]{1,2,0:T(8,128)(2,1)S(1)} %get-tuple-element.18), channel_id=1, replica_groups=mesh['data'=16] {'data'}, dimensions={0}, use_global_device_ids=true | all-gather | bytes 29920 | tf_op jit(solution)/shard_map/all_gather | solution.py:56
  646.9 0.7 reshape.101
  649.0 31.5 %all-reduce = bf16[5120]{0:T(1024)(128)(2,1)S(1)} all-reduce(bf16[5120]{0:T(1024)(128)(2,1)S(1)} %dynamic-update-slice), channel_id=1, replica_groups=mesh['data'=16] {'data'}, use_global_device_ids=true, to_apply=%add | all-reduce | flops 5120 | bytes 20480
  680.6 0.6 reshape.99
  681.2 11.6 %all-gather.4.cloned.1.call-done = bf16[4,1638400]{1,0:T(4,128)(2,1)} async-done(((bf16[4,102400]{1,0:T(4,128)(2,1)}), bf16[4,1638400]{1,0:T(4,128)(2,1)}) %all-gather.4.cloned.1.call-update) | async-done | bytes 13107216 | tf_op jit(solution)/shard_map/all_gather | solution.py:56
  692.8 110.1 %all-gather.6.cloned.1.call-done = bf16[2,6553600]{1,0:T(2,128)(2,1)} async-done(((bf16[2,409600]{1,0:T(2,128)(2,1)}), bf16[2,6553600]{1,0:T(2,128)(2,1)}) %all-gather.6.cloned.1.call-update) | async-done | bytes 26214416 | tf_op jit(solution)/shard_map/all_gather | solution.py:56
  802.9 10.1 %copy.42 = bf16[4,1638400]{1,0:T(4,128)(2,1)} copy(bf16[4,1638400]{1,0:T(4,128)(2,1)} %all-gather.4.cloned.1.call-done) | data formatting | bytes 26214400
  813.1 21.0 %copy.43 = bf16[2,6553600]{1,0:T(2,128)(2,1)} copy(bf16[2,6553600]{1,0:T(2,128)(2,1)} %all-gather.6.cloned.1.call-done) | data formatting | bytes 52428800
  (52 shorter events, 4.2 us)
Async XLA Ops:
  10.0 10.7 %all-to-all-start.2 = ((bf16[16,2,160]{2,1,0:T(2,128)(2,1)}), bf16[16,2,160]{2,1,0:T(2,128)(2,1)S(1)}, u32[]{:S(2)}, u32[]{:S(2)}) async-start(bf16[16,2,160]{2,1,0:T(2,128)(2,1)} %reshape.105), calls=%async_computation.2 | async-start | bytes 32768 | tf_op jit(solution)/shard_map/all_to_all | solution.py:39
  177.1 322.0 %all-to-all-start.1 = ((bf16[2,16,409600]{2,0,1:T(2,128)(2,1)}), bf16[2,16,409600]{2,0,1:T(2,128)(2,1)}, u32[]{:S(2)}, u32[]{:S(2)}) async-start(bf16[2,16,409600]{2,0,1:T(2,128)(2,1)} %bitcast.20), calls=%async_computation.1 | async-start | bytes 52428800 | tf_op jit(solution)/shard_map/all_to_all | solution.py:39
  184.7 508.1 %all-gather.4.cloned.1.call-start = ((), (), s32[]{:S(2)}) async-start(), calls=%async_computation.4 | async-start | bytes 13926400 | tf_op jit(solution)/shard_map/all_gather | solution.py:56
  204.9 1.2 copy-start
  564.3 16.6 %copy-start.1 = (f32[4,102400]{1,0:T(4,128)S(1)}, f32[4,102400]{1,0:T(4,128)}, u32[]{:S(2)}) copy-start(f32[4,102400]{1,0:T(4,128)} %copy-done) | copy-start | bytes 4915204
  564.3 16.6 %copy-start.3 = (f32[4,102400]{1,0:T(4,128)S(1)}, f32[4,102400]{1,0:T(4,128)}, u32[]{:S(2)}) copy-start(f32[4,102400]{1,0:T(4,128)} %param.20) | copy-start | bytes 4915204
  564.3 16.6 %copy-start.4 = (f32[4,102400]{1,0:T(4,128)S(1)}, f32[4,102400]{1,0:T(4,128)}, u32[]{:S(2)}) copy-start(f32[4,102400]{1,0:T(4,128)} %param.24) | copy-start | bytes 4915204
  564.3 16.6 %copy-start.5 = (f32[4,102400]{1,0:T(4,128)S(1)}, f32[4,102400]{1,0:T(4,128)}, u32[]{:S(2)}) copy-start(f32[4,102400]{1,0:T(4,128)} %param.28) | copy-start | bytes 4915204
  580.9 4.8 copy-start.6
  580.9 4.8 copy-start.9
  580.9 4.8 copy-start.10
  580.9 5.0 copy-start.11
  580.9 5.0 copy-start.12
  581.0 5.0 copy-start.13
  585.9 46.1 %copy-start.7 = (f32[11,80]{1,0:T(8,128)}, f32[11,80]{1,0:T(8,128)S(1)}, u32[]{:S(2)}) copy-start(f32[11,80]{1,0:T(8,128)S(1)} %get-tuple-element.72) | copy-start | bytes 10564
  585.9 46.1 %copy-start.8 = (f32[11,80]{1,0:T(8,128)}, f32[11,80]{1,0:T(8,128)S(1)}, u32[]{:S(2)}) copy-start(f32[11,80]{1,0:T(8,128)S(1)} %get-tuple-element.76) | copy-start | bytes 10564
  621.3 4.2 copy-start.2
  625.4 177.5 %all-gather.6.cloned.1.call-start = ((), (), s32[]{:S(2)}) async-start(), calls=%async_computation.5 | async-start | bytes 27852800 | tf_op jit(solution)/shard_map/all_gather | solution.py:56
Sparse Core Ops, SparseCore 0:
  625.5 67.2 all-gather.3
  695.6 107.2 all-gather.5
where the time goes:
time: 842 us; the launch traced here: 841 us
  waiting for transfers between devices  418 us (50%)
  blocking collectives  268 us (32%)
  other arithmetic  85.6 us (10%)
  local copies, waits for them, and re-layouts  38.5 us (5%)
  between operations  18.3 us (2%)
  starting transfers between devices  13.1 us (2%)
    all_to_all x2, waiting for transfers between devices, local_step(): received = lax.all_to_all(by_owner, 'data', 1, 1, tiled=True)  296 us
    all_to_all x2, blocking collectives, local_step(): received = lax.all_to_all(by_owner, 'data', 1, 1, tiled=True)  156 us
    all_gather x2, waiting for transfers between devices, local_step(): lax.all_gather(new_weight.astype(jnp.bfloat16), 'data', axis=1, tiled=True)  122 us
    reduce_sum x4, other arithmetic, local_step(): mean_grads.append(jnp.sum(received, axis=1, dtype=jnp.float32) / group_size)  43.4 us
    unnamed x39, local copies, waits for them, and re-layouts  35.5 us
    psum x1, blocking collectives, local_step(): lax.psum(local_square, 'data')  33.1 us
    psum x1, blocking collectives, local_step(): norm_sums = lax.psum(part_sums, 'data')  32.6 us
    unnamed x1, blocking collectives  31.5 us
  transfers between devices with their start and end apart: 4, of which 4 were waited for; matrix products, arithmetic and copies ran while one was open for 4% of the time, Pallas kernels for 0%

commit v1 on v0

v1 whole, which is shorter than its diff:
```python
import functools

import jax
import jax.numpy as jnp
from jax import lax
from jax.experimental import pallas as pl
from jax.experimental.pallas import tpu as pltpu
from jax.sharding import PartitionSpec as P

STEP_NUMBER = 10
LEARN_RATE = 0.04
BETA_FIRST = 0.9
BETA_SECOND = 0.999
EPSILON = 1e-6
WEIGHT_DECAY = 0.01
MAX_NORM = 1.0

MESH = pl.DeviceIdType.MESH
GROUP = 16
LANES = 128
ATTN_ROWS = 3200
MLP_ROWS = 6400
THIRD = 3200
PIECE = 320
PIECES = THIRD // PIECE
LOAD_SLOTS = 3
SEND_SLOTS = 4
SMALL_ROWS = 16
CORE = 1
ORDERS = ((2, 4, 8), (4, 8, 2), (8, 2, 4))
UNITS = (
    (0, (0, 1, 2), ()),
    (0, (0, 1), ()),
    (0, (0, 2), ()),
    (1, (1, 2), (0,)),
    (0, (0,), ()),
    (1, (1,), (1,)),
    (2, (2,), (2, 3)),
    (None, (), (4, 5, 6)),
)


def flip(index, width):
    return index + width * (1 - 2 * ((index // width) % 2))


def flip_all(index, widths):
    for width in widths:
        index = flip(index, width)
    return index


def meet_everyone(me):
    barrier = pltpu.get_barrier_semaphore()

    def signal(step, carry):
        pl.semaphore_signal(barrier, inc=1, device_id=((me + step) % GROUP,), device_id_type=MESH)
        return carry

    lax.fori_loop(1, GROUP, signal, 0)
    pl.semaphore_wait(barrier, GROUP - 1)


def tile_to_everyone(me, source_of, slots, send_sems, recv_sems, begin):
    def copy(step):
        return pltpu.make_async_remote_copy(
            source_of((me + step) % GROUP), slots.at[me], send_sems.at[step], recv_sems.at[step],
            device_id=((me + step) % GROUP,), device_id_type=MESH)

    def arrival(step):
        return pltpu.make_async_remote_copy(
            source_of((me + step) % GROUP), slots.at[(me - step + GROUP) % GROUP], send_sems.at[step], recv_sems.at[step],
            device_id=((me + step) % GROUP,), device_id_type=MESH)

    def start(step, carry):
        copy(step).start()
        return carry

    def finish(step, carry):
        arrival(step).wait()
        return carry

    lax.fori_loop(1, GROUP, start if begin else finish, 0)


def scatter_kernel(grad_attn, grad_mlp, grad_small, sums, small_sums, total, pair_raw, landed,
                   raw_own, raw_pair, partial, outgoing, square_sum, small_slots, square_slots,
                   load_sems, send_sems, pair_send_first, pair_recv_first, pair_send, pair_recv, land_sems,
                   small_send, small_recv, square_send, square_recv, local_sem):
    me = lax.axis_index("data")
    twin = flip(me, CORE)
    meet_everyone(me)

    def grad_of(third, owner, row, count):
        if third == 0:
            return grad_attn.at[owner, pl.ds(row, count)]
        return grad_mlp.at[owner, pl.ds(row + (third - 1) * THIRD, count)]

    def owner_of(unit, third):
        return flip_all(me, [ORDERS[third][place] for place in UNITS[unit][1]])

    def pair_first(third, piece):
        rows = piece * PIECE
        return pltpu.make_async_remote_copy(
            grad_of(third, flip(owner_of(0, third), CORE), rows, PIECE), pair_raw.at[0, third, pl.ds(rows, PIECE)],
            pair_send_first.at[third, piece], pair_recv_first.at[third, piece], device_id=(twin,), device_id_type=MESH)

    def pair_copy(unit, third):
        return pltpu.make_async_remote_copy(
            grad_of(third, flip(owner_of(unit, third), CORE), 0, THIRD), pair_raw.at[unit, third],
            pair_send.at[unit, third], pair_recv.at[unit, third], device_id=(twin,), device_id_type=MESH)

    def start_first(piece, carry):
        for third in range(3):
            pair_first(third, piece).start()
        return carry

    lax.fori_loop(0, PIECES, start_first, 0)
    for unit in range(1, 8):
        for third in range(3):
            pair_copy(unit, third).start()
    own_small = pltpu.make_async_copy(grad_small.at[me], small_slots.at[me], local_sem)
    own_small.start()
    tile_to_everyone(me, lambda owner: grad_small.at[owner], small_slots, small_send, small_recv, True)
    square_sum[...] = jnp.zeros_like(square_sum)

    def loads(unit, third, piece):
        rows = piece * PIECE
        slot = (unit * PIECES + piece) % LOAD_SLOTS
        copies = [
            pltpu.make_async_copy(grad_of(third, owner_of(unit, third), rows, PIECE), raw_own.at[slot, third], load_sems.at[slot, third, 0]),
            pltpu.make_async_copy(pair_raw.at[unit, third, pl.ds(rows, PIECE)], raw_pair.at[slot, third], load_sems.at[slot, third, 1]),
        ]
        for place, source in enumerate(UNITS[unit][2]):
            copies.append(pltpu.make_async_copy(
                landed.at[source, third, pl.ds(rows, PIECE)], partial.at[slot, third, place], load_sems.at[slot, third, 2 + place]))
        return copies

    def send(unit, third, piece):
        rows = piece * PIECE
        slot = (unit * PIECES + piece) % SEND_SLOTS
        to = flip(me, ORDERS[third][UNITS[unit][0]])
        return pltpu.make_async_remote_copy(
            outgoing.at[slot, third], landed.at[unit, third, pl.ds(rows, PIECE)],
            send_sems.at[slot, third], land_sems.at[unit, third, piece], device_id=(to,), device_id_type=MESH)

    def begin(unit, piece):
        for third in range(3):
            if unit == 0:
                pair_first(third, piece).wait_recv()
            else:
                @pl.when(piece == 0)
                def _():
                    pair_copy(unit, third).wait_recv()
            for source in UNITS[unit][2]:
                send(source, third, piece).wait_recv()
            for copy in loads(unit, third, piece):
                copy.start()

    ahead = LOAD_SLOTS - 1
    for piece in range(ahead):
        begin(0, piece)

    for unit in range(8):
        def work(piece, carry, unit=unit):
            @pl.when(piece + ahead < PIECES)
            def _():
                begin(unit, piece + ahead)
            if unit < 7:
                @pl.when(piece + ahead >= PIECES)
                def _():
                    begin(unit + 1, piece + ahead - PIECES)
            slot = (unit * PIECES + piece) % LOAD_SLOTS
            out_slot = (unit * PIECES + piece) % SEND_SLOTS
            for third in range(3):
                for copy in loads(unit, third, piece):
                    copy.wait()
                value = raw_own[slot, third].astype(jnp.float32) + raw_pair[slot, third].astype(jnp.float32)
                for place in range(len(UNITS[unit][2])):
                    value = value + partial[slot, third, place]
                if unit < 7:
                    if unit == 0:
                        @pl.when(piece >= SEND_SLOTS)
                        def _():
                            send(unit, third, piece).wait_send()
                    else:
                        send(unit, third, piece).wait_send()
                    outgoing[out_slot, third] = value
                    send(unit, third, piece).start()
                else:
                    value = value * (1.0 / GROUP)
                    sums[pl.ds(pl.multiple_of(third * THIRD + piece * PIECE, PIECE), PIECE)] = value
                    square_sum[...] += jnp.sum((value * value).reshape(PIECE // 8, 8, LANES), axis=0)
            return carry

        lax.fori_loop(0, PIECES, work, 0)

    own_small.wait()
    tile_to_everyone(me, lambda owner: grad_small.at[owner], small_slots, small_send, small_recv, False)
    small = jnp.sum(small_slots[...].astype(jnp.float32), axis=0) * (1.0 / GROUP)
    small_sums[...] = small
    squares = square_sum[...] + (small * small)[0:8] + (small * small)[8:16]
    square_sum[...] = squares
    square_slots[me] = squares
    tile_to_everyone(me, lambda owner: square_sum, square_slots, square_send, square_recv, True)
    for slot in range(SEND_SLOTS):
        for third in range(3):
            send(6, third, slot).wait_send()

    def drain(piece, carry):
        for third in range(3):
            pair_first(third, piece).wait_send()
        return carry

    lax.fori_loop(0, PIECES, drain, 0)
    for unit in range(1, 8):
        for third in range(3):
            pair_copy(unit, third).wait_send()
    tile_to_everyone(me, lambda owner: square_sum, square_slots, square_send, square_recv, False)
    total[...] = jnp.full((8, LANES), jnp.sum(square_slots[...]), jnp.float32)


def reduce_scatter(grad_attn, grad_mlp, grad_small):
    rows = ATTN_ROWS + MLP_ROWS
    anywhere = pl.BlockSpec(memory_space=pl.ANY)
    inside = pl.BlockSpec(memory_space=pltpu.VMEM)
    dma = pltpu.SemaphoreType.DMA
    return pl.pallas_call(
        scatter_kernel,
        name="scatter",
        out_shape=(
            jax.ShapeDtypeStruct((rows, LANES), jnp.float32),
            jax.ShapeDtypeStruct((SMALL_ROWS, LANES), jnp.float32),
            jax.ShapeDtypeStruct((8, LANES), jnp.float32),
            jax.ShapeDtypeStruct((8, 3, THIRD, LANES), jnp.bfloat16),
            jax.ShapeDtypeStruct((7, 3, THIRD, LANES), jnp.float32),
        ),
        in_specs=[anywhere] * 3,
        out_specs=(inside, inside, inside, anywhere, anywhere),
        scratch_shapes=[
            pltpu.VMEM((LOAD_SLOTS, 3, PIECE, LANES), jnp.bfloat16),
            pltpu.VMEM((LOAD_SLOTS, 3, PIECE, LANES), jnp.bfloat16),
            pltpu.VMEM((LOAD_SLOTS, 3, 3, PIECE, LANES), jnp.float32),
            pltpu.VMEM((SEND_SLOTS, 3, PIECE, LANES), jnp.float32),
            pltpu.VMEM((8, LANES), jnp.float32),
            pltpu.VMEM((GROUP, SMALL_ROWS, LANES), jnp.bfloat16),
            pltpu.VMEM((GROUP, 8, LANES), jnp.float32),
            dma((LOAD_SLOTS, 3, 5)),
            dma((SEND_SLOTS, 3)),
            dma((3, PIECES)),
            dma((3, PIECES)),
            dma((8, 3)),
            dma((8, 3)),
            dma((7, 3, PIECES)),
            dma((GROUP,)),
            dma((GROUP,)),
            dma((GROUP,)),
            dma((GROUP,)),
            dma(()),
        ],
        compiler_params=pltpu.CompilerParams(collective_id=0, has_side_effects=True),
    )(grad_attn, grad_mlp, grad_small)[:3]


def gather_kernel(part_sums, weight, update, small_weight, small_update,
                  all_attn, all_mlp, all_small, ratios,
                  fresh, fresh_small, slots,
                  tile_send, tile_recv, small_send, small_recv, own_send, link_send, link_recv, twin_send, twin_recv):
    me = lax.axis_index("data")
    twin = flip(me, CORE)
    meet_everyone(me)
    slots[me] = part_sums[...]
    tile_to_everyone(me, lambda owner: part_sums, slots, tile_send, tile_recv, True)
    tile_to_everyone(me, lambda owner: part_sums, slots, tile_send, tile_recv, False)
    sums = jnp.sum(slots[...], axis=0)
    lane = lax.broadcasted_iota(jnp.int32, (8, LANES), 1)

    def column(place):
        return jnp.sum(jnp.where(lane == place, sums, 0.0), axis=1, keepdims=True)

    def same_tensor(value, rows):
        total = value
        for shift in range(rows, 8, rows):
            total = total + pltpu.roll(value, shift, 0)
        return total

    def wide_rows(value):
        row = lax.broadcasted_iota(jnp.int32, (8, 1), 0)
        mine = jnp.logical_and(row >= 3, row < 6)
        return jnp.where(mine, jnp.sum(jnp.where(mine, value, 0.0), axis=0, keepdims=True), value)

    def spread(value):
        return jnp.broadcast_to(value, (8, LANES))

    def ratio(weights, updates):
        safe = jnp.where(updates > 0.0, updates, 1.0)
        return jnp.sqrt(weights) / jnp.sqrt(safe)

    ratio_attn = ratio(same_tensor(spread(column(0)), 4), same_tensor(spread(column(1)), 4))
    ratio_mlp = ratio(same_tensor(spread(column(2)), 2), same_tensor(spread(column(3)), 2))
    ratio_low = ratio(spread(column(4)), spread(column(5)))
    ratio_high = ratio(spread(wide_rows(column(6))), spread(wide_rows(column(7))))
    ratios[0] = ratio_attn
    ratios[1] = ratio_mlp
    ratios[2] = ratio_low
    ratios[3] = ratio_high

    def place_of(third, owner):
        if third == 0:
            return all_attn.at[owner]
        return all_mlp.at[owner, pl.ds((third - 1) * THIRD, THIRD)]

    def link(third, stage, hops, source=None):
        number = {0: 0, 1: 1, 2: 3}[stage] + {(): 0, (0,): 1, (1,): 2, (0, 1): 3}[hops]
        to = flip(me, ORDERS[third][stage])
        owner = flip_all(me, [ORDERS[third][hop] for hop in hops])
        place = place_of(third, owner)
        return pltpu.make_async_remote_copy(
            place if source is None else source, place, link_send.at[third, number], link_recv.at[third, number],
            device_id=(to,), device_id_type=MESH)

    def landed(third, stage, hops):
        number = {0: 0, 1: 1, 2: 3}[stage] + {(): 0, (0,): 1, (1,): 2, (0, 1): 3}[hops]
        owner = flip_all(flip(me, ORDERS[third][stage]), [ORDERS[third][hop] for hop in hops])
        place = place_of(third, owner)
        return pltpu.make_async_remote_copy(
            place, place, link_send.at[third, number], link_recv.at[third, number],
            device_id=(flip(me, ORDERS[third][stage]),), device_id_type=MESH)

    def to_twin(third, number, hops, source=None):
        owner = flip_all(me, [ORDERS[third][hop] for hop in hops])
        place = place_of(third, owner)
        return pltpu.make_async_remote_copy(
            place if source is None else source, place, twin_send.at[third, number], twin_recv.at[third, number],
            device_id=(twin,), device_id_type=MESH)

    def from_twin(third, number, hops):
        owner = flip_all(twin, [ORDERS[third][hop] for hop in hops])
        place = place_of(third, owner)
        return pltpu.make_async_remote_copy(
            place, place, twin_send.at[third, number], twin_recv.at[third, number],
            device_id=(twin,), device_id_type=MESH)

    own = []
    for third in range(3):
        scale = LEARN_RATE * (ratio_attn if third == 0 else ratio_mlp)

        def refresh(piece, carry, third=third, scale=scale):
            rows = pl.ds(pl.multiple_of(third * THIRD + piece * PIECE, PIECE), PIECE)
            old = weight[rows].reshape(PIECE // 8, 8, LANES)
            step = update[rows].reshape(PIECE // 8, 8, LANES)
            fresh[rows] = (old - scale[None] * step).reshape(PIECE, LANES).astype(jnp.bfloat16)
            return carry

        lax.fori_loop(0, PIECES, refresh, 0)
        source = fresh.at[pl.ds(third * THIRD, THIRD)]
        link(third, 0, (), source).start()
    for stage in (1, 2):
        for third in range(3):
            link(third, stage, (), fresh.at[pl.ds(third * THIRD, THIRD)]).start()
    for third in range(3):
        source = fresh.at[pl.ds(third * THIRD, THIRD)]
        to_twin(third, 0, (), source).start()
        copy = pltpu.make_async_copy(source, place_of(third, me), own_send.at[third])
        copy.start()
        own.append(copy)
    low = small_weight[0:8] - LEARN_RATE * ratio_low * small_update[0:8]
    high = small_weight[8:16] - LEARN_RATE * ratio_high * small_update[8:16]
    fresh_small[...] = jnp.concatenate([low, high], axis=0).astype(jnp.bfloat16)
    own_small = pltpu.make_async_copy(fresh_small, all_small.at[me], own_send.at[3])
    own_small.start()
    tile_to_everyone(me, lambda owner: fresh_small, all_small, small_send, small_recv, True)

    arrivals = (
        (0, (), ((1, (0,)), (2, (0,)))),
        (1, (), ((2, (1,)),)),
        (2, (), ()),
        (1, (0,), ((2, (0, 1)),)),
        (2, (0,), ()),
        (2, (1,), ()),
        (2, (0, 1), ()),
    )
    number = 1
    sent = []
    for stage, hops, forwards in arrivals:
        for third in range(3):
            landed(third, stage, hops).wait_recv()
            for forward in forwards:
                copy = link(third, *forward)
                copy.start()
                sent.append(copy)
            to_twin(third, number, (stage,) + hops).start()
        number += 1
    number = 0
    for hops in ((),) + tuple((stage,) + hops for stage, hops, _ in arrivals):
        for third in range(3):
            copy = from_twin(third, number, hops)
            copy.wait_recv()
            to_twin(third, number, hops).wait_send()
        number += 1
    for third in range(3):
        for stage in range(3):
            link(third, stage, ()).wait_send()
    for copy in sent:
        copy.wait_send()
    for copy in own:
        copy.wait()
    own_small.wait()
    tile_to_everyone(me, lambda owner: fresh_small, all_small, small_send, small_recv, False)


def all_gather(part_sums, weight, update, small_weight, small_update):
    anywhere = pl.BlockSpec(memory_space=pl.ANY)
    inside = pl.BlockSpec(memory_space=pltpu.VMEM)
    dma = pltpu.SemaphoreType.DMA
    rows = ATTN_ROWS + MLP_ROWS
    return pl.pallas_call(
        gather_kernel,
        name="gather",
        out_shape=(
            jax.ShapeDtypeStruct((GROUP, ATTN_ROWS, LANES), jnp.bfloat16),
            jax.ShapeDtypeStruct((GROUP, MLP_ROWS, LANES), jnp.bfloat16),
            jax.ShapeDtypeStruct((GROUP, SMALL_ROWS, LANES), jnp.bfloat16),
            jax.ShapeDtypeStruct((4, 8, LANES), jnp.float32),
        ),
        in_specs=[inside] * 5,
        out_specs=(anywhere, anywhere, anywhere, inside),
        scratch_shapes=[
            pltpu.VMEM((rows, LANES), jnp.bfloat16),
            pltpu.VMEM((SMALL_ROWS, LANES), jnp.bfloat16),
            pltpu.VMEM((GROUP, 8, LANES), jnp.float32),
            dma((GROUP,)), dma((GROUP,)), dma((GROUP,)), dma((GROUP,)),
            dma((4,)), dma((3, 7)), dma((3, 7)), dma((3, 8)), dma((3, 8)),
        ],
        compiler_params=pltpu.CompilerParams(collective_id=1, has_side_effects=True),
    )(part_sums, weight, update, small_weight, small_update)


def linear(bank):
    rows, length = bank.shape
    return bank.reshape(rows, length // LANES, LANES).transpose(1, 0, 2).reshape(rows * length // LANES, LANES)


def banked(flat, rows):
    blocks = flat.size // (rows * LANES)
    return flat.reshape(blocks, rows, LANES).transpose(1, 0, 2).reshape(rows, blocks * LANES)


def pack_small(wide, vec):
    lead = [(0, 0)] * (wide.ndim - 1)
    vec_rows = jnp.pad(vec, lead + [(0, 0), (0, LANES - 80)])
    wide_rows = jnp.pad(wide, lead + [(0, 64)]).reshape(wide.shape[:-1] + (3, LANES))
    return jnp.concatenate([vec_rows, jnp.pad(wide_rows, lead + [(0, 2), (0, 0)])], axis=-2)


def unpack_small(packed):
    lead = packed.shape[:-2]
    return packed[..., 11:14, :].reshape(lead + (3 * LANES,))[..., :320], packed[..., :11, :80]


def solution(mesh):
    grad_spec = P("data", None, None)
    shard_spec = P(None, "data")
    full_spec = P(None, None)

    def direction(mean_grad, weight, first, second, clip_coef):
        clipped = clip_coef * mean_grad
        new_first = BETA_FIRST * first + (1.0 - BETA_FIRST) * clipped
        new_second = BETA_SECOND * second + (1.0 - BETA_SECOND) * (clipped * clipped)
        update = (new_first / (1.0 - BETA_FIRST ** STEP_NUMBER)) / (jnp.sqrt(new_second / (1.0 - BETA_SECOND ** STEP_NUMBER)) + EPSILON) + WEIGHT_DECAY * weight
        return update, new_first, new_second

    def local_step(*banks):
        grads = banks[0:4]
        attn_grad = linear(grads[0][0]).reshape(GROUP, ATTN_ROWS, LANES)
        mlp_grad = linear(grads[1][0]).reshape(GROUP, MLP_ROWS, LANES)
        small_grad = pack_small(grads[2][0].reshape(GROUP, 320), grads[3][0].reshape(11, GROUP, 80).transpose(1, 0, 2))
        sums, small_sums, total = reduce_scatter(attn_grad, mlp_grad, small_grad)
        clip_coef = jnp.minimum(1.0, MAX_NORM / jnp.sqrt(total[0, 0]))
        states = []
        for first in (4, 8, 12):
            attn, mlp, wide, vec = banks[first:first + 4]
            states.append((jnp.concatenate([linear(attn), linear(mlp)], axis=0), pack_small(wide[0], vec)))
        (weight, small_weight), (first, small_first), (second, small_second) = states
        update, new_first, new_second = direction(sums, weight, first, second, clip_coef)
        small_update, small_new_first, small_new_second = direction(small_sums, small_weight, small_first, small_second, clip_coef)

        def tile_sum(value):
            return jnp.sum((value * value).reshape(-1, 8, LANES), axis=(0, 2))

        columns = [
            tile_sum(weight[:ATTN_ROWS]), tile_sum(update[:ATTN_ROWS]), tile_sum(weight[ATTN_ROWS:]), tile_sum(update[ATTN_ROWS:]),
            tile_sum(small_weight[:8]), tile_sum(small_update[:8]), tile_sum(small_weight[8:]), tile_sum(small_update[8:]),
        ]
        part_sums = jnp.pad(jnp.stack(columns, axis=1), ((0, 0), (0, LANES - 8)))
        all_attn, all_mlp, all_small, ratios = all_gather(part_sums, weight, update, small_weight, small_update)

        def stepped(weight, update, ratio):
            return (weight.reshape(-1, 8, LANES) - LEARN_RATE * ratio[None] * update.reshape(-1, 8, LANES)).reshape(weight.shape)

        new_attn = stepped(weight[:ATTN_ROWS], update[:ATTN_ROWS], ratios[0])
        new_mlp = stepped(weight[ATTN_ROWS:], update[ATTN_ROWS:], ratios[1])
        new_small = small_weight - LEARN_RATE * ratios[2:4].reshape(SMALL_ROWS, LANES) * small_update
        replica_wide, replica_vec = unpack_small(all_small)
        replicas = [
            banked(all_attn, 4), banked(all_mlp, 2), replica_wide.reshape(1, 5120),
            replica_vec.transpose(1, 0, 2).reshape(11, 1280),
        ]
        outs = list(replicas)
        for attn, mlp, small in (
            (new_attn, new_mlp, new_small),
            (new_first[:ATTN_ROWS], new_first[ATTN_ROWS:], small_new_first),
            (new_second[:ATTN_ROWS], new_second[ATTN_ROWS:], small_new_second),
        ):
            wide, vec = unpack_small(small)
            outs += [banked(attn, 4), banked(mlp, 2), wide[None], vec]
        return tuple(outs)

    return jax.shard_map(local_step, mesh=mesh, in_specs=(grad_spec,) * 4 + (shard_spec,) * 12, out_specs=(full_spec,) * 4 + (shard_spec,) * 12, check_vma=False)
```

time: 842 us -> 508 us (0.60)
  waiting for transfers between devices: 418 us -> 0 us
  Pallas kernels: 0 us -> 408 us
  blocking collectives: 268 us -> 0 us
  other arithmetic: 85.6 us -> 38.4 us
  local copies, waits for them, and re-layouts: 38.5 us -> 58.6 us
  between operations: 18.3 us -> 1.66 us
  starting transfers between devices: 13.1 us -> 0 us
    pallas_call x0 -> x2, Pallas kernels: none -> 408 us  [the longest x1 266 us: reduce_scatter(): pl.pallas_call(scatter_kernel, name='scatter', out_shape=(jax.ShapeDtypeS...]
    all_to_all x2 -> x0, waiting for transfers between devices: 296 us -> none  [local_step(): received = lax.all_to_all(by_owner, 'data', 1, 1, tiled=True)]
    all_to_all x2 -> x0, blocking collectives: 156 us -> none  [local_step(): received = lax.all_to_all(by_owner, 'data', 1, 1, tiled=True)]
    all_gather x2 -> x0, waiting for transfers between devices: 122 us -> none  [local_step(): lax.all_gather(new_weight.astype(jnp.bfloat16), 'data', axis=1, tiled=True)]
    psum x2 -> x0, blocking collectives: 65.7 us -> none  [the longest x1 33.1 us: local_step(): lax.psum(local_square, 'data')]
    reduce_sum x12 -> x8, other arithmetic: 72.7 us -> 12.4 us  [tile_sum(): return jnp.sum((value * value).reshape(-1, 8, LANES), axis=(0, 2))]
    unnamed x1 -> x0, blocking collectives: 31.5 us -> none
    all_gather x1 -> x0, blocking collectives: 14.2 us -> none  [local_step(): lax.all_gather(new_weight.astype(jnp.bfloat16), 'data', axis=1, tiled=True)]
  transfers between devices with their start and end apart: 4 -> 0, of which waited for: 4 -> 0; matrix products, arithmetic and copies ran while one was open for 4% -> 0% of each run, Pallas kernels for 0% -> 0%
where the time goes in v1:
time: 508 us; the launch traced here: 507 us
  Pallas kernels  408 us (80%)
  local copies, waits for them, and re-layouts  58.6 us (12%)
  other arithmetic  38.4 us (8%)
    pallas_call x1, Pallas kernels, reduce_scatter(): pl.pallas_call(scatter_kernel, name='scatter', out_shape=(jax.ShapeDtypeS...  266 us
    pallas_call x1, Pallas kernels, all_gather(): pl.pallas_call(gather_kernel, name='gather', out_shape=(jax.ShapeDtypeStr...  142 us
    unnamed x41, local copies, waits for them, and re-layouts  33.6 us
    reduce_sum x8, other arithmetic, tile_sum(): return jnp.sum((value * value).reshape(-1, 8, LANES), axis=(0, 2))  12.4 us
    add x2, other arithmetic, direction(): new_first / (1.0 - BETA_FIRST ** STEP_NUMBER) / (jnp.sqrt(new_second / (1...  12.1 us

profile of v1, /device:TPU:0, one launch (start us, length us, event | category | flops | bytes accessed | tf_op | source)
XLA Modules:
  0.0 506.9 jit_solution(12616512131146191073)
XLA Ops:
  0.6 0.9 reshape_squeeze.14
  1.6 0.8 reduce.16
  2.5 0.7 fusion.8.grad_small
  3.2 266.2 %scatter.1 = (f32[9600,128]{1,0:T(8,128)}, f32[16,128]{1,0:T(8,128)}, f32[8,128]{1,0:T(8,128)}, bf16[8,3,3200,128]{3,2,1,0:T(8,128)(2,1)}, f32[7,3,3200,128]{3,2,1,0:T(8,128)}) custom-call(bf16[16,3200,128]{2,1,0:T(8,128)(2,1)} %bitcast.143, bf16[16,6400,128]{2,1,0:T(8,128)(2,1)} %bitcast.140, bf16[16,16,128]{2,1,0:T(8,128)(2,1)} %fusion.8.grad_small), custom_call_target="tpu_custom_call" | custom-call | tf_op jit(solution)/shard_map/scatter/pallas_call | solution.py:228
  269.3 1.2 slice.80
  271.4 0.7 multiply_add_fusion.1
  272.6 11.4 %multiply_add_fusion = (f32[9600,128]{1,0:T(8,128)S(1)}, f32[9600,128]{1,0:T(8,128)}, f32[9600,128]{1,0:T(8,128)}, f32[9600,128]{1,0:T(8,128)}) fusion(f32[6400,128]{1,0:T(8,128)S(1)} %bitcast.139, f32[3200,128]{1,0:T(8,128)} %bitcast.142, f32[9600,128]{1,0:T(8,128)} %get-tuple-element.24, f32[]{:T(128)} %bitcast.16, f32[6400,128]{1,0:T(8,128)} %bitcast.151, ...), kind=kLoop, calls=%fused_computation.5 | loop fusion | flops 20889600 | bytes 39321604 | tf_op jit(solution)/shard_map/add | solution.py:470
  284.0 2.3 copy-done
  286.3 2.5 fusion.21
  288.8 1.0 reduce_sum.110
  289.8 1.1 reduce_sum.111
  291.0 3.0 fusion.22
  294.3 6.6 %fusion.3 = f32[3200,2]{1,0:T(8,128)} fusion(f32[2,409600]{1,0:T(2,128)S(1)} %copy-done.1), kind=kLoop, calls=%fused_computation.9 | loop fusion | flops 1632000 | bytes 3302400 | tf_op jit(solution)/shard_map/reduce_sum | solution.py:489
  300.9 2.6 reduce_sum.107
  303.5 1.1 reduce_sum.108
  304.7 3.1 fusion.4
  307.8 1.1 reduce_sum.82
  309.4 0.6 pad.58.part_sums
  310.0 142.1 %gather.1 = (bf16[16,3200,128]{2,1,0:T(8,128)(2,1)}, bf16[16,6400,128]{2,1,0:T(8,128)(2,1)}, bf16[16,16,128]{2,1,0:T(8,128)(2,1)}, f32[4,8,128]{2,1,0:T(8,128)}) custom-call(f32[8,128]{1,0:T(8,128)} %pad.58.part_sums, f32[9600,128]{1,0:T(8,128)} %get-tuple-element.43.weight, f32[9600,128]{1,0:T(8,128)} %copy-done, f32[16,128]{1,0:T(8,128)} %copy-done.8, ...), custom_call_target="tpu_custom_call" | custom-call | tf_op jit(solution)/shard_map/gather/pallas_call | solution.py:417
  452.1 0.9 fusion.13
  452.9 0.6 broadcast_in_dim.9
  453.5 0.7 multiply_bitcast_fusion
  454.4 3.7 fusion.2
  458.2 1.7 fusion.5
  460.0 0.7 reshape.196
  460.8 0.7 reshape.195
  462.6 3.8 slice.115
  466.5 3.8 slice.119
  470.3 2.7 slice.114
  473.0 2.7 slice.118
  475.7 10.1 %copy.89 = bf16[4,1638400]{1,0:T(4,128)(2,1)} copy(bf16[4,1638400]{1,0:T(4,128)(2,1)} %bitcast.144) | data formatting | bytes 26214400
  485.8 21.0 %copy.90 = bf16[2,6553600]{1,0:T(2,128)(2,1)} copy(bf16[2,6553600]{1,0:T(2,128)(2,1)} %bitcast.141) | data formatting | bytes 52428800
  (72 shorter events, 3.1 us)
Async XLA Ops:
  3.1 268.1 %copy-start.10 = (f32[11,80]{1,0:T(8,128)S(1)}, f32[11,80]{1,0:T(8,128)}, u32[]{:S(2)}) copy-start(f32[11,80]{1,0:T(8,128)} %param.23) | copy-start | bytes 10564
  3.1 268.1 %copy-start.16 = (f32[1,320]{1,0:T(1,128)S(1)}, f32[1,320]{1,0:T(1,128)}, u32[]{:S(2)}) copy-start(f32[1,320]{1,0:T(1,128)} %param.22) | copy-start | bytes 3844
  3.1 268.2 %copy-start.17 = (f32[1,320]{1,0:T(1,128)S(1)}, f32[1,320]{1,0:T(1,128)}, u32[]{:S(2)}) copy-start(f32[1,320]{1,0:T(1,128)} %param.30) | copy-start | bytes 3844
  3.1 268.2 %copy-start.18 = (f32[1,320]{1,0:T(1,128)S(1)}, f32[1,320]{1,0:T(1,128)}, u32[]{:S(2)}) copy-start(f32[1,320]{1,0:T(1,128)} %param.26) | copy-start | bytes 3844
  3.1 268.2 %copy-start.14 = (f32[11,80]{1,0:T(8,128)S(1)}, f32[11,80]{1,0:T(8,128)}, u32[]{:S(2)}) copy-start(f32[11,80]{1,0:T(8,128)} %param.27) | copy-start | bytes 10564
  3.2 268.2 %copy-start.15 = (f32[11,80]{1,0:T(8,128)S(1)}, f32[11,80]{1,0:T(8,128)}, u32[]{:S(2)}) copy-start(f32[11,80]{1,0:T(8,128)} %param.31) | copy-start | bytes 10564
  3.2 269.4 %copy-start.1 = (f32[2,409600]{1,0:T(2,128)S(1)}, f32[2,409600]{1,0:T(2,128)}, u32[]{:S(2)}) copy-start(f32[2,409600]{1,0:T(2,128)} %param.21) | copy-start | bytes 9830404
  272.1 11.9 %copy-start.5 = (f32[16,128]{1,0:T(8,128)}, f32[16,128]{1,0:T(8,128)S(1)}, u32[]{:S(2)}) copy-start(f32[16,128]{1,0:T(8,128)S(1)} %get-tuple-element.32.small_update) | copy-start | bytes 24580
  272.1 11.8 %copy-start.8 = (f32[16,128]{1,0:T(8,128)}, f32[16,128]{1,0:T(8,128)S(1)}, u32[]{:S(2)}) copy-start(f32[16,128]{1,0:T(8,128)S(1)} %get-tuple-element.35.small_weight) | copy-start | bytes 24580
  272.2 189.3 %copy-start.11 = (f32[16,128]{1,0:T(8,128)}, f32[16,128]{1,0:T(8,128)S(1)}, u32[]{:S(2)}) copy-start(f32[16,128]{1,0:T(8,128)S(1)} %get-tuple-element.33) | copy-start | bytes 24580
  272.2 189.3 %copy-start.12 = (f32[16,128]{1,0:T(8,128)}, f32[16,128]{1,0:T(8,128)S(1)}, u32[]{:S(2)}) copy-start(f32[16,128]{1,0:T(8,128)S(1)} %get-tuple-element.34) | copy-start | bytes 24580
  284.0 2.3 copy-start
  310.0 142.1 %copy-start.6 = (f32[16,128]{1,0:T(8,128)S(1)}, f32[16,128]{1,0:T(8,128)}, u32[]{:S(2)}) copy-start(f32[16,128]{1,0:T(8,128)} %copy-done.5) | copy-start | bytes 24580
  310.0 142.1 %copy-start.9 = (f32[16,128]{1,0:T(8,128)S(1)}, f32[16,128]{1,0:T(8,128)}, u32[]{:S(2)}) copy-start(f32[16,128]{1,0:T(8,128)} %copy-done.8) | copy-start | bytes 24580
  452.0 2.4 copy-start.3
  452.9 5.2 %copy-start.13 = (f32[16,128]{1,0:T(8,128)}, f32[16,128]{1,0:T(8,128)S(1)}, u32[]{:S(2)}) copy-start(f32[16,128]{1,0:T(8,128)S(1)} %fusion.13) | copy-start | bytes 24580
  454.4 3.8 copy-start.2
  454.4 3.8 copy-start.4
  458.1 1.9 copy-start.7

commit v2 on v1

--- a/solution.py
+++ b/solution.py
@@ -20,12 +20,21 @@
 LANES = 128
 ATTN_ROWS = 3200
 MLP_ROWS = 6400
+ROWS = ATTN_ROWS + MLP_ROWS
 THIRD = 3200
 PIECE = 320
 PIECES = THIRD // PIECE
 LOAD_SLOTS = 3
 SEND_SLOTS = 4
 SMALL_ROWS = 16
+BLOCK = 64
+CHUNK = 640
+CHUNKS = THIRD // CHUNK
+OUT_SLOTS = 4
+SCATTER_VMEM = 20 * 2 ** 20
+UPDATE_VMEM = 8 * 2 ** 20
+GATHER_VMEM = 2 * 2 ** 20
+FINISH_VMEM = 3 * 2 ** 20
 CORE = 1
 ORDERS = ((2, 4, 8), (4, 8, 2), (8, 2, 4))
 UNITS = (
@@ -221,7 +230,6 @@
 
 
 def reduce_scatter(grad_attn, grad_mlp, grad_small):
-    rows = ATTN_ROWS + MLP_ROWS
     anywhere = pl.BlockSpec(memory_space=pl.ANY)
     inside = pl.BlockSpec(memory_space=pltpu.VMEM)
     dma = pltpu.SemaphoreType.DMA
@@ -229,11 +237,11 @@
         scatter_kernel,
         name="scatter",
         out_shape=(
-            jax.ShapeDtypeStruct((rows, LANES), jnp.float32),
-            jax.ShapeDtypeStruct((SMALL_ROWS, LANES), jnp.float32),
-            jax.ShapeDtypeStruct((8, LANES), jnp.float32),
-            jax.ShapeDtypeStruct((8, 3, THIRD, LANES), jnp.bfloat16),
-            jax.ShapeDtypeStruct((7, 3, THIRD, LANES), jnp.float32),
+            pltpu.VMEM((ROWS, LANES), jnp.float32),
+            pltpu.VMEM((SMALL_ROWS, LANES), jnp.float32),
+            pltpu.VMEM((8, LANES), jnp.float32),
+            pltpu.HBM((8, 3, THIRD, LANES), jnp.bfloat16),
+            pltpu.HBM((7, 3, THIRD, LANES), jnp.float32),
         ),
         in_specs=[anywhere] * 3,
         out_specs=(inside, inside, inside, anywhere, anywhere),
@@ -258,13 +266,128 @@
             dma((GROUP,)),
             dma(()),
         ],
-        compiler_params=pltpu.CompilerParams(collective_id=0, has_side_effects=True),
-    )(grad_attn, grad_mlp, grad_small)[:3]
-
-
-def gather_kernel(part_sums, weight, update, small_weight, small_update,
-                  all_attn, all_mlp, all_small, ratios,
-                  fresh, fresh_small, slots,
+        compiler_params=pltpu.CompilerParams(collective_id=0, has_side_effects=True, vmem_limit_bytes=SCATTER_VMEM),
+    )(*[pltpu.with_memory_space_constraint(grad, pltpu.HBM) for grad in (grad_attn, grad_mlp)], grad_small)[:3]
+
+
+def bank_part(third, attn, mlp):
+    return (attn, 0) if third == 0 else (mlp, (third - 1) * THIRD)
+
+
+def update_kernel(sums, small_sums, total, weight_attn, weight_mlp, first_attn, first_mlp, second_attn, second_mlp,
+                  small_weight, small_first, small_second,
+                  update, small_update, part_sums, new_first_attn, new_first_mlp, new_second_attn, new_second_mlp,
+                  small_new_first, small_new_second,
+                  first_out, second_out, out_sems):
+    clip_coef = jnp.minimum(1.0, MAX_NORM / jnp.sqrt(total[0:1, :]))
+
+    def direction(mean_grad, weight, first, second):
+        clipped = clip_coef * mean_grad
+        new_first = BETA_FIRST * first + (1.0 - BETA_FIRST) * clipped
+        new_second = BETA_SECOND * second + (1.0 - BETA_SECOND) * (clipped * clipped)
+        root = jnp.sqrt(new_second * (1.0 / (1.0 - BETA_SECOND ** STEP_NUMBER))) + EPSILON
+        return (new_first * (1.0 / (1.0 - BETA_FIRST ** STEP_NUMBER))) / root + WEIGHT_DECAY * weight, new_first, new_second
+
+    def tile_sum(value):
+        return jnp.sum((value * value).reshape(-1, 8, LANES), axis=0)
+
+    def copies(third, chunk):
+        slot = (third * CHUNKS + chunk) % OUT_SLOTS
+        first_to, base = bank_part(third, new_first_attn, new_first_mlp)
+        second_to, _ = bank_part(third, new_second_attn, new_second_mlp)
+        rows = pl.ds(base + chunk * CHUNK, CHUNK)
+        return (
+            pltpu.make_async_copy(first_out.at[slot], first_to.at[rows], out_sems.at[slot, 0]),
+            pltpu.make_async_copy(second_out.at[slot], second_to.at[rows], out_sems.at[slot, 1]),
+        )
+
+    totals = []
+    for third in range(3):
+        weight, base = bank_part(third, weight_attn, weight_mlp)
+        first, _ = bank_part(third, first_attn, first_mlp)
+        second, _ = bank_part(third, second_attn, second_mlp)
+
+        def work(chunk, carry, third=third, weight=weight, first=first, second=second, base=base):
+            slot = (third * CHUNKS + chunk) % OUT_SLOTS
+            place = third * CHUNKS + chunk
+
+            @pl.when(place >= OUT_SLOTS)
+            def _():
+                for copy in copies(third, chunk):
+                    copy.wait()
+
+            def block(step, carry):
+                squares_weight, squares_update = carry
+                inner = pl.multiple_of(step * BLOCK, BLOCK)
+                rows = pl.ds(pl.multiple_of(base + chunk * CHUNK + inner, BLOCK), BLOCK)
+                old = weight[rows]
+                new_update, new_first, new_second = direction(
+                    sums[pl.ds(pl.multiple_of(third * THIRD + chunk * CHUNK + inner, BLOCK), BLOCK)], old, first[rows], second[rows])
+                first_out[slot, pl.ds(inner, BLOCK)] = new_first
+                second_out[slot, pl.ds(inner, BLOCK)] = new_second
+                update[pl.ds(pl.multiple_of(third * THIRD + chunk * CHUNK + inner, BLOCK), BLOCK)] = new_update
+                return squares_weight + tile_sum(old), squares_update + tile_sum(new_update)
+
+            carry = lax.fori_loop(0, CHUNK // BLOCK, block, carry)
+            for copy in copies(third, chunk):
+                copy.start()
+            return carry
+
+        zero = jnp.zeros((8, LANES), jnp.float32)
+        totals.append(lax.fori_loop(0, CHUNKS, work, (zero, zero)))
+    small, small_m, small_v = direction(small_sums[...], small_weight[...], small_first[...], small_second[...])
+    small_update[...] = small
+    small_new_first[...] = small_m
+    small_new_second[...] = small_v
+    old = small_weight[...]
+    columns = [
+        totals[0][0], totals[0][1], totals[1][0] + totals[2][0], totals[1][1] + totals[2][1],
+        (old * old)[0:8], (small * small)[0:8], (old * old)[8:16], (small * small)[8:16],
+    ]
+    lane = lax.broadcasted_iota(jnp.int32, (8, LANES), 1)
+    tile = jnp.zeros((8, LANES), jnp.float32)
+    for place, column in enumerate(columns):
+        tile = jnp.where(lane == place, jnp.sum(column, axis=1, keepdims=True), tile)
+    part_sums[...] = tile
+    for place in range(3 * CHUNKS - OUT_SLOTS, 3 * CHUNKS):
+        for copy in copies(place // CHUNKS, place % CHUNKS):
+            copy.wait()
+
+
+def resident(value):
+    return pltpu.with_memory_space_constraint(value, pltpu.VMEM)
+
+
+def update_step(sums, small_sums, total, weights, firsts, seconds, smalls):
+    anywhere = pl.BlockSpec(memory_space=pl.ANY)
+    inside = pl.BlockSpec(memory_space=pltpu.VMEM)
+    attn = pltpu.HBM((ATTN_ROWS, LANES), jnp.float32)
+    mlp = pltpu.HBM((MLP_ROWS, LANES), jnp.float32)
+    small = jax.ShapeDtypeStruct((SMALL_ROWS, LANES), jnp.float32)
+    operands = [sums, small_sums, total, *weights, *firsts, *seconds]
+    return pl.pallas_call(
+        update_kernel,
+        name="update",
+        out_shape=(
+            pltpu.VMEM((ROWS, LANES), jnp.float32),
+            pltpu.VMEM((SMALL_ROWS, LANES), jnp.float32),
+            pltpu.VMEM((8, LANES), jnp.float32),
+            attn, mlp, attn, mlp, small, small,
+        ),
+        in_specs=[inside] * 12,
+        out_specs=(inside, inside, inside, anywhere, anywhere, anywhere, anywhere, inside, inside),
+        scratch_shapes=[
+            pltpu.VMEM((OUT_SLOTS, CHUNK, LANES), jnp.float32),
+            pltpu.VMEM((OUT_SLOTS, CHUNK, LANES), jnp.float32),
+            pltpu.SemaphoreType.DMA((OUT_SLOTS, 2)),
+        ],
+        compiler_params=pltpu.CompilerParams(vmem_limit_bytes=UPDATE_VMEM),
+    )(*[resident(value) for value in operands], *smalls)
+
+
+def gather_kernel(part_sums, weight_attn, weight_mlp, update, small_weight, small_update,
+                  everything, all_small, ratios,
+                  fresh_small, slots,
                   tile_send, tile_recv, small_send, small_recv, own_send, link_send, link_recv, twin_send, twin_recv):
     me = lax.axis_index("data")
     twin = flip(me, CORE)
@@ -306,17 +429,15 @@
     ratios[3] = ratio_high
 
     def place_of(third, owner):
-        if third == 0:
-            return all_attn.at[owner]
-        return all_mlp.at[owner, pl.ds((third - 1) * THIRD, THIRD)]
-
-    def link(third, stage, hops, source=None):
+        return everything.at[owner, pl.ds(third * THIRD, THIRD)]
+
+    def link(third, stage, hops):
         number = {0: 0, 1: 1, 2: 3}[stage] + {(): 0, (0,): 1, (1,): 2, (0, 1): 3}[hops]
         to = flip(me, ORDERS[third][stage])
         owner = flip_all(me, [ORDERS[third][hop] for hop in hops])
         place = place_of(third, owner)
         return pltpu.make_async_remote_copy(
-            place if source is None else source, place, link_send.at[third, number], link_recv.at[third, number],
+            place, place, link_send.at[third, number], link_recv.at[third, number],
             device_id=(to,), device_id_type=MESH)
 
     def landed(third, stage, hops):
@@ -327,11 +448,11 @@
             place, place, link_send.at[third, number], link_recv.at[third, number],
             device_id=(flip(me, ORDERS[third][stage]),), device_id_type=MESH)
 
-    def to_twin(third, number, hops, source=None):
+    def to_twin(third, number, hops):
         owner = flip_all(me, [ORDERS[third][hop] for hop in hops])
         place = place_of(third, owner)
         return pltpu.make_async_remote_copy(
-            place if source is None else source, place, twin_send.at[third, number], twin_recv.at[third, number],
+            place, place, twin_send.at[third, number], twin_recv.at[third, number],
             device_id=(twin,), device_id_type=MESH)
 
     def from_twin(third, number, hops):
@@ -341,33 +462,28 @@
             place, place, twin_send.at[third, number], twin_recv.at[third, number],
             device_id=(twin,), device_id_type=MESH)
 
-    own = []
     for third in range(3):
         scale = LEARN_RATE * (ratio_attn if third == 0 else ratio_mlp)
-
-        def refresh(piece, carry, third=third, scale=scale):
+        weight, base = bank_part(third, weight_attn, weight_mlp)
+
+        def refresh(piece, carry, third=third, scale=scale, weight=weight, base=base):
             rows = pl.ds(pl.multiple_of(third * THIRD + piece * PIECE, PIECE), PIECE)
-            old = weight[rows].reshape(PIECE // 8, 8, LANES)
+            old = weight[pl.ds(pl.multiple_of(base + piece * PIECE, PIECE), PIECE)].reshape(PIECE // 8, 8, LANES)
             step = update[rows].reshape(PIECE // 8, 8, LANES)
-            fresh[rows] = (old - scale[None] * step).reshape(PIECE, LANES).astype(jnp.bfloat16)
+            everything[me, rows] = (old - scale[None] * step).reshape(PIECE, LANES).astype(jnp.bfloat16)
             return carry
 
         lax.fori_loop(0, PIECES, refresh, 0)
-        source = fresh.at[pl.ds(third * THIRD, THIRD)]
-        link(third, 0, (), source).start()
+        link(third, 0, ()).start()
     for stage in (1, 2):
         for third in range(3):
-            link(third, stage, (), fresh.at[pl.ds(third * THIRD, THIRD)]).start()
+            link(third, stage, ()).start()
     for third in range(3):
-        source = fresh.at[pl.ds(third * THIRD, THIRD)]
-        to_twin(third, 0, (), source).start()
-        copy = pltpu.make_async_copy(source, place_of(third, me), own_send.at[third])
-        copy.start()
-        own.append(copy)
+        to_twin(third, 0, ()).start()
     low = small_weight[0:8] - LEARN_RATE * ratio_low * small_update[0:8]
     high = small_weight[8:16] - LEARN_RATE * ratio_high * small_update[8:16]
     fresh_small[...] = jnp.concatenate([low, high], axis=0).astype(jnp.bfloat16)
-    own_small = pltpu.make_async_copy(fresh_small, all_small.at[me], own_send.at[3])
+    own_small = pltpu.make_async_copy(fresh_small, all_small.at[me], own_send)
     own_small.start()
     tile_to_everyone(me, lambda owner: fresh_small, all_small, small_send, small_recv, True)
 
@@ -403,37 +519,129 @@
             link(third, stage, ()).wait_send()
     for copy in sent:
         copy.wait_send()
-    for copy in own:
-        copy.wait()
     own_small.wait()
     tile_to_everyone(me, lambda owner: fresh_small, all_small, small_send, small_recv, False)
 
 
-def all_gather(part_sums, weight, update, small_weight, small_update):
-    anywhere = pl.BlockSpec(memory_space=pl.ANY)
+def all_gather(part_sums, weights, update, small_weight, small_update):
     inside = pl.BlockSpec(memory_space=pltpu.VMEM)
     dma = pltpu.SemaphoreType.DMA
-    rows = ATTN_ROWS + MLP_ROWS
     return pl.pallas_call(
         gather_kernel,
         name="gather",
         out_shape=(
-            jax.ShapeDtypeStruct((GROUP, ATTN_ROWS, LANES), jnp.bfloat16),
-            jax.ShapeDtypeStruct((GROUP, MLP_ROWS, LANES), jnp.bfloat16),
-            jax.ShapeDtypeStruct((GROUP, SMALL_ROWS, LANES), jnp.bfloat16),
-            jax.ShapeDtypeStruct((4, 8, LANES), jnp.float32),
+            pltpu.VMEM((GROUP, ROWS, LANES), jnp.bfloat16),
+            pltpu.VMEM((GROUP, SMALL_ROWS, LANES), jnp.bfloat16),
+            pltpu.VMEM((4, 8, LANES), jnp.float32),
         ),
-        in_specs=[inside] * 5,
-        out_specs=(anywhere, anywhere, anywhere, inside),
+        in_specs=[inside] * 6,
+        out_specs=(inside,) * 3,
         scratch_shapes=[
-            pltpu.VMEM((rows, LANES), jnp.bfloat16),
             pltpu.VMEM((SMALL_ROWS, LANES), jnp.bfloat16),
             pltpu.VMEM((GROUP, 8, LANES), jnp.float32),
             dma((GROUP,)), dma((GROUP,)), dma((GROUP,)), dma((GROUP,)),
-            dma((4,)), dma((3, 7)), dma((3, 7)), dma((3, 8)), dma((3, 8)),
+            dma(()), dma((3, 7)), dma((3, 7)), dma((3, 8)), dma((3, 8)),
         ],
-        compiler_params=pltpu.CompilerParams(collective_id=1, has_side_effects=True),
-    )(part_sums, weight, update, small_weight, small_update)
+        compiler_params=pltpu.CompilerParams(collective_id=1, has_side_effects=True, vmem_limit_bytes=GATHER_VMEM),
+    )(*[resident(value) for value in (part_sums, *weights, update)], small_weight, small_update)
+
+
+def write_kernel(everything, replica_attn, replica_mlp, attn_sems, mlp_sems):
+    writes = []
+    for owner in range(GROUP):
+        writes.append(pltpu.make_async_copy(
+            everything.at[owner, pl.ds(0, ATTN_ROWS)], replica_attn.at[pl.ds(owner * ATTN_ROWS, ATTN_ROWS)], attn_sems.at[owner]))
+        writes.append(pltpu.make_async_copy(
+            everything.at[owner, pl.ds(ATTN_ROWS, MLP_ROWS)], replica_mlp.at[pl.ds(owner * MLP_ROWS, MLP_ROWS)], mlp_sems.at[owner]))
+    for copy in writes:
+        copy.start()
+    for copy in writes:
+        copy.wait()
+
+
+def write_replica(everything):
+    anywhere = pl.BlockSpec(memory_space=pl.ANY)
+    dma = pltpu.SemaphoreType.DMA
+    return pl.pallas_call(
+        write_kernel,
+        name="write",
+        out_shape=(
+            pltpu.HBM((GROUP * ATTN_ROWS, LANES), jnp.bfloat16),
+            pltpu.HBM((GROUP * MLP_ROWS, LANES), jnp.bfloat16),
+        ),
+        in_specs=[pl.BlockSpec(memory_space=pltpu.VMEM)],
+        out_specs=(anywhere,) * 2,
+        scratch_shapes=[dma((GROUP,)), dma((GROUP,))],
+        compiler_params=pltpu.CompilerParams(vmem_limit_bytes=FINISH_VMEM),
+    )(resident(everything))
+
+
+def finish_kernel(weight_attn, weight_mlp, update, ratios, all_small, small_weight, small_update,
+                  new_attn, new_mlp, replica_small, new_small,
+                  fresh, fresh_small, weight_sems, small_sems):
+    writes = []
+    for tile in range(2):
+        rows = pl.ds(8 * tile, 8)
+        fresh_small[rows] = small_weight[rows] - LEARN_RATE * ratios[2 + tile] * small_update[rows]
+    for place, (source, to) in enumerate(((all_small, replica_small), (fresh_small, new_small))):
+        copy = pltpu.make_async_copy(source, to, small_sems.at[place])
+        copy.start()
+        writes.append(copy)
+    def write(third, chunk):
+        slot = (third * CHUNKS + chunk) % OUT_SLOTS
+        to, base = bank_part(third, new_attn, new_mlp)
+        return pltpu.make_async_copy(fresh.at[slot], to.at[pl.ds(base + chunk * CHUNK, CHUNK)], weight_sems.at[slot])
+
+    for third in range(3):
+        scale = LEARN_RATE * ratios[0 if third == 0 else 1]
+        weight, base = bank_part(third, weight_attn, weight_mlp)
+
+        def work(chunk, carry, third=third, scale=scale, weight=weight, base=base):
+            slot = (third * CHUNKS + chunk) % OUT_SLOTS
+
+            @pl.when(third * CHUNKS + chunk >= OUT_SLOTS)
+            def _():
+                write(third, chunk).wait()
+
+            def refresh(block, inner):
+                start = chunk * CHUNK + block * BLOCK
+                old = weight[pl.ds(pl.multiple_of(base + start, BLOCK), BLOCK)].reshape(BLOCK // 8, 8, LANES)
+                step = update[pl.ds(pl.multiple_of(third * THIRD + start, BLOCK), BLOCK)].reshape(BLOCK // 8, 8, LANES)
+                fresh[slot, pl.ds(pl.multiple_of(block * BLOCK, BLOCK), BLOCK)] = (old - scale[None] * step).reshape(BLOCK, LANES)
+                return inner
+
+            lax.fori_loop(0, CHUNK // BLOCK, refresh, 0)
+            write(third, chunk).start()
+            return carry
+
+        lax.fori_loop(0, CHUNKS, work, 0)
+    for place in range(3 * CHUNKS - OUT_SLOTS, 3 * CHUNKS):
+        write(place // CHUNKS, place % CHUNKS).wait()
+    for copy in writes:
+        copy.wait()
+
+
+def finish(all_small, weights, update, small_weight, small_update, ratios):
+    anywhere = pl.BlockSpec(memory_space=pl.ANY)
+    inside = pl.BlockSpec(memory_space=pltpu.VMEM)
+    dma = pltpu.SemaphoreType.DMA
+    return pl.pallas_call(
+        finish_kernel,
+        name="finish",
+        out_shape=(
+            pltpu.HBM((ATTN_ROWS, LANES), jnp.float32),
+            pltpu.HBM((MLP_ROWS, LANES), jnp.float32),
+            pltpu.HBM((GROUP, SMALL_ROWS, LANES), jnp.bfloat16),
+            pltpu.HBM((SMALL_ROWS, LANES), jnp.float32),
+        ),
+        in_specs=[inside] * 7,
+        out_specs=(anywhere,) * 4,
+        scratch_shapes=[
+            pltpu.VMEM((OUT_SLOTS, CHUNK, LANES), jnp.float32), pltpu.VMEM((SMALL_ROWS, LANES), jnp.float32),
+            dma((OUT_SLOTS,)), dma((2,)),
+        ],
+        compiler_params=pltpu.CompilerParams(vmem_limit_bytes=FINISH_VMEM),
+    )(*[resident(value) for value in (*weights, update, ratios, all_small)], small_weight, small_update)
 
 
 def linear(bank):
@@ -463,54 +671,33 @@
     shard_spec = P(None, "data")
     full_spec = P(None, None)
 
-    def direction(mean_grad, weight, first, second, clip_coef):
-        clipped = clip_coef * mean_grad
-        new_first = BETA_FIRST * first + (1.0 - BETA_FIRST) * clipped
-        new_second = BETA_SECOND * second + (1.0 - BETA_SECOND) * (clipped * clipped)
-        update = (new_first / (1.0 - BETA_FIRST ** STEP_NUMBER)) / (jnp.sqrt(new_second / (1.0 - BETA_SECOND ** STEP_NUMBER)) + EPSILON) + WEIGHT_DECAY * weight
-        return update, new_first, new_second
-
     def local_step(*banks):
         grads = banks[0:4]
         attn_grad = linear(grads[0][0]).reshape(GROUP, ATTN_ROWS, LANES)
         mlp_grad = linear(grads[1][0]).reshape(GROUP, MLP_ROWS, LANES)
         small_grad = pack_small(grads[2][0].reshape(GROUP, 320), grads[3][0].reshape(11, GROUP, 80).transpose(1, 0, 2))
-        sums, small_sums, total = reduce_scatter(attn_grad, mlp_grad, small_grad)
-        clip_coef = jnp.minimum(1.0, MAX_NORM / jnp.sqrt(total[0, 0]))
-        states = []
+        states, smalls = [], []
         for first in (4, 8, 12):
             attn, mlp, wide, vec = banks[first:first + 4]
-            states.append((jnp.concatenate([linear(attn), linear(mlp)], axis=0), pack_small(wide[0], vec)))
-        (weight, small_weight), (first, small_first), (second, small_second) = states
-        update, new_first, new_second = direction(sums, weight, first, second, clip_coef)
-        small_update, small_new_first, small_new_second = direction(small_sums, small_weight, small_first, small_second, clip_coef)
-
-        def tile_sum(value):
-            return jnp.sum((value * value).reshape(-1, 8, LANES), axis=(0, 2))
-
-        columns = [
-            tile_sum(weight[:ATTN_ROWS]), tile_sum(update[:ATTN_ROWS]), tile_sum(weight[ATTN_ROWS:]), tile_sum(update[ATTN_ROWS:]),
-            tile_sum(small_weight[:8]), tile_sum(small_update[:8]), tile_sum(small_weight[8:]), tile_sum(small_update[8:]),
-        ]
-        part_sums = jnp.pad(jnp.stack(columns, axis=1), ((0, 0), (0, LANES - 8)))
-        all_attn, all_mlp, all_small, ratios = all_gather(part_sums, weight, update, small_weight, small_update)
-
-        def stepped(weight, update, ratio):
-            return (weight.reshape(-1, 8, LANES) - LEARN_RATE * ratio[None] * update.reshape(-1, 8, LANES)).reshape(weight.shape)
-
-        new_attn = stepped(weight[:ATTN_ROWS], update[:ATTN_ROWS], ratios[0])
-        new_mlp = stepped(weight[ATTN_ROWS:], update[ATTN_ROWS:], ratios[1])
-        new_small = small_weight - LEARN_RATE * ratios[2:4].reshape(SMALL_ROWS, LANES) * small_update
+            states.append((linear(attn), linear(mlp)))
+            smalls.append(pack_small(wide[0], vec))
+        small_grad, *smalls = lax.optimization_barrier((small_grad, *smalls))
+        sums, small_sums, total = reduce_scatter(attn_grad, mlp_grad, small_grad)
+        update, small_update, part_sums, *moments = update_step(sums, small_sums, total, *states, smalls)
+        everything, all_small, ratios = all_gather(part_sums, states[0], update, smalls[0], small_update)
+        replica_attn, replica_mlp = write_replica(everything)
+        replica_attn, all_small = lax.optimization_barrier((replica_attn, all_small))
+        new_attn, new_mlp, all_small, new_small = finish(
+            all_small, states[0], update, smalls[0], small_update, ratios)
         replica_wide, replica_vec = unpack_small(all_small)
-        replicas = [
-            banked(all_attn, 4), banked(all_mlp, 2), replica_wide.reshape(1, 5120),
+        outs = [
+            banked(replica_attn, 4), banked(replica_mlp, 2), replica_wide.reshape(1, 5120),
             replica_vec.transpose(1, 0, 2).reshape(11, 1280),
         ]
-        outs = list(replicas)
         for attn, mlp, small in (
             (new_attn, new_mlp, new_small),
-            (new_first[:ATTN_ROWS], new_first[ATTN_ROWS:], small_new_first),
-            (new_second[:ATTN_ROWS], new_second[ATTN_ROWS:], small_new_second),
+            (moments[0], moments[1], moments[4]),
+            (moments[2], moments[3], moments[5]),
         ):
             wide, vec = unpack_small(small)
             outs += [banked(attn, 4), banked(mlp, 2), wide[None], vec]

time: 508 us -> 440 us (0.87)
  local copies, waits for them, and re-layouts: 58.6 us -> 7.91 us
  other arithmetic: 38.4 us -> 4.36 us
  Pallas kernels: 408 us -> 426 us
    unnamed x41 -> x13, local copies, waits for them, and re-layouts: 33.6 us -> 0.04 us
    pallas_call x2 -> x5, Pallas kernels: 408 us -> 426 us  [the longest x1 265 us: reduce_scatter(): pl.pallas_call(scatter_kernel, name='scatter', out_shape=(pltpu.VMEM((ROW...]
    slice x5 -> x0, local copies, waits for them, and re-layouts: 14.3 us -> none  [the longest x1 3.84 us: local_step(): new_first[ATTN_ROWS:]]
    reduce_sum x8 -> x0, other arithmetic: 12.4 us -> none  [tile_sum(): return jnp.sum((value * value).reshape(-1, 8, LANES), axis=(0, 2))]
    add x2 -> x0, other arithmetic: 12.1 us -> none  [direction(): new_first / (1.0 - BETA_FIRST ** STEP_NUMBER) / (jnp.sqrt(new_second / (1...]
    slice x2 -> x0, other arithmetic: 5.45 us -> none  [the longest x1 2.96 us: local_step(): update[:ATTN_ROWS]]
    reshape x2 -> x0, other arithmetic: 5.42 us -> none  [banked(): flat.reshape(blocks, rows, LANES).transpose(1, 0, 2)]
where the time goes in v2:
time: 440 us; the launch traced here: 439 us
  Pallas kernels  426 us (97%)
  local copies, waits for them, and re-layouts  7.91 us (2%)
    pallas_call x1, Pallas kernels, reduce_scatter(): pl.pallas_call(scatter_kernel, name='scatter', out_shape=(pltpu.VMEM((ROW...  265 us
    pallas_call x1, Pallas kernels, all_gather(): pl.pallas_call(gather_kernel, name='gather', out_shape=(pltpu.VMEM((GROUP...  138 us
    pallas_call x1, Pallas kernels, write_replica(): pl.pallas_call(write_kernel, name='write', out_shape=(pltpu.HBM((GROUP *...  12.9 us

profile of v2, /device:TPU:0, one launch (start us, length us, event | category | flops | bytes accessed | tf_op | source)
XLA Modules:
  0.0 439.4 jit_solution(2257471686304127224)
XLA Ops:
  0.6 0.7 reduce.3
  1.4 0.7 reduce.2
  2.1 0.7 select_maximum_fusion
  2.8 0.9 reshape_squeeze.14
  3.7 0.8 reduce
  4.5 0.1 reshape_squeeze.15
  4.7 0.7 reduce.1
  5.4 0.7 select_maximum_fusion.2.small_weight
  6.1 0.0 copy-start.2
  6.1 0.0 copy-start.3
  6.1 0.0 copy-start.4
  6.1 0.0 copy-start.5
  6.1 264.9 %scatter.1 = (f32[9600,128]{1,0:T(8,128)S(1)}, f32[16,128]{1,0:T(8,128)S(1)}, f32[8,128]{1,0:T(8,128)S(1)}, bf16[8,3,3200,128]{3,2,1,0:T(8,128)(2,1)}, f32[7,3,3200,128]{3,2,1,0:T(8,128)}) custom-call(bf16[16,3200,128]{2,1,0:T(8,128)(2,1)} %bitcast.119, bf16[16,6400,128]{2,1,0:T(8,128)(2,1)} %bitcast.118, bf16[16,16,128]{2,1,0:T(8,128)(2,1)S(1)} %fusion.2.grad_small), custom_call_target="tpu_custom_call" | custom-call | tf_op jit(solution)/shard_map/scatter/pallas_call | solution.py:236
  271.1 0.0 copy-done
  271.1 0.0 copy-done.1
  271.1 0.0 copy-done.2
  271.1 0.0 copy-done.3
  271.1 0.0 copy-done.4
  271.1 7.4 %update.1 = (f32[9600,128]{1,0:T(8,128)S(1)}, f32[16,128]{1,0:T(8,128)S(1)}, f32[8,128]{1,0:T(8,128)S(1)}, f32[3200,128]{1,0:T(8,128)}, f32[6400,128]{1,0:T(8,12...) custom-call(f32[9600,128]{1,0:T(8,128)S(1)} %get-tuple-element.44.sums, ...), custom_call_target="tpu_custom_call" | custom-call | tf_op jit(solution)/shard_map/update/pallas_call | solution.py:368
  278.6 137.5 %gather.1 = (bf16[16,9600,128]{2,1,0:T(8,128)(2,1)S(1)}, bf16[16,16,128]{2,1,0:T(8,128)(2,1)S(1)}, f32[4,8,128]{2,1,0:T(8,128)S(1)}) custom-call(f32[8,128]{1,0:T(8,128)S(1)} %get-tuple-element.50.part_sums, f32[3200,128]{1,0:T(8,128)S(1)} %bitcast.112, f32[6400,128]{1,0:T(8,128)S(1)} %bitcast.109, f32[9600,128]{1,0:T(8,128)S(1)} %get-tuple-element.51.update, ...), custom_call_target="tpu_custom_call" | custom-call | tf_op jit(solution)/shard_map/gather/pallas_call | solution.py:529
  416.1 12.9 %write.1 = (bf16[51200,128]{1,0:T(8,128)(2,1)}, bf16[102400,128]{1,0:T(8,128)(2,1)}) custom-call(bf16[16,9600,128]{2,1,0:T(8,128)(2,1)S(1)} %get-tuple-element.53.everything), custom_call_target="tpu_custom_call" | custom-call | tf_op jit(solution)/shard_map/write/pallas_call | solution.py:565
  429.0 3.5 finish.1
  432.5 0.8 slice_bitcast_fusion
  433.4 0.7 reshape.168
  434.1 0.8 slice.36
  434.9 0.7 reshape.167
  435.6 0.7 slice_bitcast_fusion.3
  436.3 0.6 broadcast_in_dim.9
  436.8 0.7 slice_bitcast_fusion.2
  437.5 0.6 broadcast_in_dim.10
  438.1 0.7 slice_bitcast_fusion.1
  438.8 0.6 broadcast_in_dim.11
  (12 shorter events, 0.1 us)
Async XLA Ops:
  6.1 265.0 %copy-start = (f32[2,409600]{1,0:T(2,128)S(1)}, f32[2,409600]{1,0:T(2,128)}, u32[]{:S(2)}) copy-start(f32[2,409600]{1,0:T(2,128)} %param.21) | copy-start | bytes 9830404
  6.1 265.0 %copy-start.1 = (f32[4,102400]{1,0:T(4,128)S(1)}, f32[4,102400]{1,0:T(4,128)}, u32[]{:S(2)}) copy-start(f32[4,102400]{1,0:T(4,128)} %param.20) | copy-start | bytes 4915204
  6.1 265.0 %copy-start.2 = (f32[2,409600]{1,0:T(2,128)S(1)}, f32[2,409600]{1,0:T(2,128)}, u32[]{:S(2)}) copy-start(f32[2,409600]{1,0:T(2,128)} %param.25) | copy-start | bytes 9830404
  6.1 265.0 %copy-start.3 = (f32[2,409600]{1,0:T(2,128)S(1)}, f32[2,409600]{1,0:T(2,128)}, u32[]{:S(2)}) copy-start(f32[2,409600]{1,0:T(2,128)} %param.29) | copy-start | bytes 9830404
  6.1 265.0 %copy-start.4 = (f32[4,102400]{1,0:T(4,128)S(1)}, f32[4,102400]{1,0:T(4,128)}, u32[]{:S(2)}) copy-start(f32[4,102400]{1,0:T(4,128)} %param.24) | copy-start | bytes 4915204
  6.1 265.0 %copy-start.5 = (f32[4,102400]{1,0:T(4,128)S(1)}, f32[4,102400]{1,0:T(4,128)}, u32[]{:S(2)}) copy-start(f32[4,102400]{1,0:T(4,128)} %param.28) | copy-start | bytes 4915204

commit v3 on v2

--- a/solution.py
+++ b/solution.py
@@ -18,6 +18,15 @@
 MESH = pl.DeviceIdType.MESH
 GROUP = 16
 LANES = 128
+TILE = (8, LANES)
+THIRDS = range(3)
+VECS = 11
+VEC_SHARE = 80
+VEC = 1280
+WIDE = 5120
+WIDE_PARTS = ((0, LANES), (1, LANES), (2, 64))
+WIDE_SHARE = 320
+MIB = 2 ** 20
 ATTN_ROWS = 3200
 MLP_ROWS = 6400
 ROWS = ATTN_ROWS + MLP_ROWS
@@ -28,13 +37,15 @@
 SEND_SLOTS = 4
 SMALL_ROWS = 16
 BLOCK = 64
+PARTS = 4
+LAST = THIRD // PARTS
 CHUNK = 640
 CHUNKS = THIRD // CHUNK
 OUT_SLOTS = 4
-SCATTER_VMEM = 20 * 2 ** 20
-UPDATE_VMEM = 8 * 2 ** 20
-GATHER_VMEM = 2 * 2 ** 20
-FINISH_VMEM = 3 * 2 ** 20
+SCATTER_VMEM = 30 * MIB
+UPDATE_VMEM = 8 * MIB
+GATHER_VMEM = 2 * MIB
+FINISH_VMEM = 3 * MIB
 CORE = 1
 ORDERS = ((2, 4, 8), (4, 8, 2), (8, 2, 4))
 UNITS = (
@@ -49,6 +60,9 @@
 )
 
 
+ARRIVALS = [(0, ()), (1, ()), (2, ()), (1, (0,)), (2, (0,)), (2, (1,))]
+
+
 def flip(index, width):
     return index + width * (1 - 2 * ((index // width) % 2))
 
@@ -92,10 +106,83 @@
     lax.fori_loop(1, GROUP, start if begin else finish, 0)
 
 
-def scatter_kernel(grad_attn, grad_mlp, grad_small, sums, small_sums, total, pair_raw, landed,
+def small_places(packed, wide, vec):
+    places = [(packed.at[pl.ds(0, VECS), pl.ds(0, VEC_SHARE)], vec)]
+    for part, width in WIDE_PARTS:
+        places.append((packed.at[pl.ds(VECS + part, 1), pl.ds(0, width)], wide.at[:, pl.ds(LANES * part, width)]))
+    return places
+
+
+def pack_rows(wide, vec, packed):
+    packed[...] = jnp.zeros_like(packed)
+    for inner, outer in small_places(packed, wide, vec):
+        inner[...] = outer[...]
+
+
+def unpack_rows(packed, wide, vec):
+    for inner, outer in small_places(packed, wide, vec):
+        outer[...] = inner[...]
+
+
+def shares_from(wide, vec, wide_rows, vec_rows, packed):
+    wide_rows[...] = jnp.zeros_like(wide_rows)
+    wide_rows[:1] = wide[...].astype(jnp.float32)
+    vec_rows[...] = jnp.zeros_like(vec_rows)
+    vec_rows[:VECS] = vec[...].astype(jnp.float32)
+    packed[...] = jnp.zeros_like(packed)
+
+    def window(rows, start):
+        block, shift = start // LANES * LANES, start % LANES
+        value = rows[:, block:block + LANES]
+        if shift == 0:
+            return value
+        lane = lax.broadcasted_iota(jnp.int32, value.shape, 1)
+        value = pltpu.roll(value, LANES - shift, 1)
+        if block + LANES == rows.shape[1]:
+            return value
+        after = pltpu.roll(rows[:, block + LANES:block + 2 * LANES], LANES - shift, 1)
+        return jnp.where(lane < LANES - shift, value, after)
+
+    lane = lax.broadcasted_iota(jnp.int32, (SMALL_ROWS, LANES), 1)
+    for owner in range(GROUP):
+        packed[owner] = jnp.where(lane < VEC_SHARE, window(vec_rows, VEC_SHARE * owner), 0.0)
+        for part, width in WIDE_PARTS:
+            value = window(wide_rows, WIDE_SHARE * owner + LANES * part)
+            packed[owner, pl.ds(VECS + part, 1)] = jnp.where(lane[:1] < width, value[:1], 0.0)
+
+
+def shares_to(shares, wide, vec, wide_rows, pair):
+    lane = lax.broadcasted_iota(jnp.int32, (SMALL_ROWS, LANES), 1)
+    low = lax.broadcasted_iota(jnp.int32, (1, LANES), 1) < 64
+    for block in range(VEC // LANES):
+        value = jnp.zeros((SMALL_ROWS, LANES), jnp.float32)
+        for owner in range(GROUP):
+            begin, end = max(VEC_SHARE * owner, LANES * block), min(VEC_SHARE * (owner + 1), LANES * (block + 1))
+            if begin < end:
+                shift = (VEC_SHARE * owner - LANES * block) % LANES
+                moved = shares[owner].astype(jnp.float32)
+                if shift:
+                    moved = pltpu.roll(moved, shift, 1)
+                inside = jnp.logical_and(lane >= begin - LANES * block, lane < end - LANES * block)
+                value = jnp.where(inside, moved, value)
+        vec[:, LANES * block:LANES * (block + 1)] = value[:VECS].astype(jnp.bfloat16)
+    for place in range(GROUP // 2):
+        pair[0] = shares[2 * place].astype(jnp.float32)
+        pair[1] = pltpu.roll(shares[2 * place + 1].astype(jnp.float32), 64, 1)
+        even, odd = [[pair[half, pl.ds(VECS + part, 1)] for part, _ in WIDE_PARTS] for half in range(2)]
+        blocks = [
+            even[0], even[1], jnp.where(low, even[2], odd[0]), jnp.where(low, odd[0], odd[1]), jnp.where(low, odd[1], odd[2]),
+        ]
+        for number, value in enumerate(blocks):
+            wide_rows[:1, pl.ds(LANES * (len(blocks) * place + number), LANES)] = value
+    wide[...] = wide_rows[:1].astype(jnp.bfloat16)
+
+
+def scatter_kernel(grad_attn, grad_mlp, grad_wide, grad_vec, sums, small_sums, total, pair_raw, landed,
                    raw_own, raw_pair, partial, outgoing, square_sum, small_slots, square_slots,
+                   pair_near, landed_near, wide_raw, vec_raw, wide_rows, vec_rows, packed, small_shares,
                    load_sems, send_sems, pair_send_first, pair_recv_first, pair_send, pair_recv, land_sems,
-                   small_send, small_recv, square_send, square_recv, local_sem):
+                   small_send, small_recv, square_send, square_recv, local_sems):
     me = lax.axis_index("data")
     twin = flip(me, CORE)
     meet_everyone(me)
@@ -111,38 +198,38 @@
     def pair_first(third, piece):
         rows = piece * PIECE
         return pltpu.make_async_remote_copy(
-            grad_of(third, flip(owner_of(0, third), CORE), rows, PIECE), pair_raw.at[0, third, pl.ds(rows, PIECE)],
+            grad_of(third, flip(owner_of(0, third), CORE), rows, PIECE), pair_near.at[third, pl.ds(rows, PIECE)],
             pair_send_first.at[third, piece], pair_recv_first.at[third, piece], device_id=(twin,), device_id_type=MESH)
 
     def pair_copy(unit, third):
         return pltpu.make_async_remote_copy(
-            grad_of(third, flip(owner_of(unit, third), CORE), 0, THIRD), pair_raw.at[unit, third],
+            grad_of(third, flip(owner_of(unit, third), CORE), 0, THIRD), pair_raw.at[unit - 1, third],
             pair_send.at[unit, third], pair_recv.at[unit, third], device_id=(twin,), device_id_type=MESH)
 
     def start_first(piece, carry):
-        for third in range(3):
+        for third in THIRDS:
             pair_first(third, piece).start()
         return carry
 
     lax.fori_loop(0, PIECES, start_first, 0)
-    for unit in range(1, 8):
-        for third in range(3):
-            pair_copy(unit, third).start()
-    own_small = pltpu.make_async_copy(grad_small.at[me], small_slots.at[me], local_sem)
-    own_small.start()
-    tile_to_everyone(me, lambda owner: grad_small.at[owner], small_slots, small_send, small_recv, True)
+    own_small = (
+        pltpu.make_async_copy(grad_wide, wide_raw, local_sems.at[0]), pltpu.make_async_copy(grad_vec, vec_raw, local_sems.at[1]))
+    for copy in own_small:
+        copy.start()
     square_sum[...] = jnp.zeros_like(square_sum)
 
     def loads(unit, third, piece):
         rows = piece * PIECE
         slot = (unit * PIECES + piece) % LOAD_SLOTS
         copies = [
-            pltpu.make_async_copy(grad_of(third, owner_of(unit, third), rows, PIECE), raw_own.at[slot, third], load_sems.at[slot, third, 0]),
-            pltpu.make_async_copy(pair_raw.at[unit, third, pl.ds(rows, PIECE)], raw_pair.at[slot, third], load_sems.at[slot, third, 1]),
-        ]
+            pltpu.make_async_copy(grad_of(third, owner_of(unit, third), rows, PIECE), raw_own.at[slot, third], load_sems.at[slot, third, 0])]
+        if unit > 0:
+            copies.append(pltpu.make_async_copy(
+                pair_raw.at[unit - 1, third, pl.ds(rows, PIECE)], raw_pair.at[slot, third], load_sems.at[slot, third, 1]))
         for place, source in enumerate(UNITS[unit][2]):
-            copies.append(pltpu.make_async_copy(
-                landed.at[source, third, pl.ds(rows, PIECE)], partial.at[slot, third, place], load_sems.at[slot, third, 2 + place]))
+            if source < 6:
+                copies.append(pltpu.make_async_copy(
+                    landed.at[source, third, pl.ds(rows, PIECE)], partial.at[slot, third, place], load_sems.at[slot, third, 2 + place]))
         return copies
 
     def send(unit, third, piece):
@@ -150,19 +237,18 @@
         slot = (unit * PIECES + piece) % SEND_SLOTS
         to = flip(me, ORDERS[third][UNITS[unit][0]])
         return pltpu.make_async_remote_copy(
-            outgoing.at[slot, third], landed.at[unit, third, pl.ds(rows, PIECE)],
+            outgoing.at[slot, third], (landed.at[unit, third] if unit < 6 else landed_near.at[third]).at[pl.ds(rows, PIECE)],
             send_sems.at[slot, third], land_sems.at[unit, third, piece], device_id=(to,), device_id_type=MESH)
 
     def begin(unit, piece):
-        for third in range(3):
-            if unit == 0:
-                pair_first(third, piece).wait_recv()
-            else:
+        for third in THIRDS:
+            if unit > 0:
                 @pl.when(piece == 0)
                 def _():
                     pair_copy(unit, third).wait_recv()
             for source in UNITS[unit][2]:
-                send(source, third, piece).wait_recv()
+                if source < 6:
+                    send(source, third, piece).wait_recv()
             for copy in loads(unit, third, piece):
                 copy.start()
 
@@ -181,12 +267,21 @@
                     begin(unit + 1, piece + ahead - PIECES)
             slot = (unit * PIECES + piece) % LOAD_SLOTS
             out_slot = (unit * PIECES + piece) % SEND_SLOTS
-            for third in range(3):
+            for third in THIRDS:
                 for copy in loads(unit, third, piece):
                     copy.wait()
-                value = raw_own[slot, third].astype(jnp.float32) + raw_pair[slot, third].astype(jnp.float32)
-                for place in range(len(UNITS[unit][2])):
-                    value = value + partial[slot, third, place]
+                rows = pl.ds(pl.multiple_of(piece * PIECE, PIECE), PIECE)
+                if unit == 0:
+                    pair_first(third, piece).wait_recv()
+                    value = raw_own[slot, third].astype(jnp.float32) + pair_near[third, rows].astype(jnp.float32)
+                else:
+                    value = raw_own[slot, third].astype(jnp.float32) + raw_pair[slot, third].astype(jnp.float32)
+                for place, source in enumerate(UNITS[unit][2]):
+                    if source < 6:
+                        value = value + partial[slot, third, place]
+                    else:
+                        send(source, third, piece).wait_recv()
+                        value = value + landed_near[third, rows]
                 if unit < 7:
                     if unit == 0:
                         @pl.when(piece >= SEND_SLOTS)
@@ -200,12 +295,25 @@
                     value = value * (1.0 / GROUP)
                     sums[pl.ds(pl.multiple_of(third * THIRD + piece * PIECE, PIECE), PIECE)] = value
                     square_sum[...] += jnp.sum((value * value).reshape(PIECE // 8, 8, LANES), axis=0)
+            if unit == 0:
+                @pl.when(piece == 0)
+                def _():
+                    for later in range(1, 8):
+                        for third in THIRDS:
+                            pair_copy(later, third).start()
             return carry
 
         lax.fori_loop(0, PIECES, work, 0)
-
-    own_small.wait()
-    tile_to_everyone(me, lambda owner: grad_small.at[owner], small_slots, small_send, small_recv, False)
+        if unit == 0:
+            for copy in own_small:
+                copy.wait()
+            shares_from(wide_raw, vec_raw, wide_rows, vec_rows, packed)
+            small_shares[...] = packed[...].astype(jnp.bfloat16)
+            small_slots[me] = small_shares[me]
+        if unit == 1:
+            tile_to_everyone(me, lambda owner: small_shares.at[owner], small_slots, small_send, small_recv, True)
+
+    tile_to_everyone(me, lambda owner: small_shares.at[owner], small_slots, small_send, small_recv, False)
     small = jnp.sum(small_slots[...].astype(jnp.float32), axis=0) * (1.0 / GROUP)
     small_sums[...] = small
     squares = square_sum[...] + (small * small)[0:8] + (small * small)[8:16]
@@ -213,23 +321,23 @@
     square_slots[me] = squares
     tile_to_everyone(me, lambda owner: square_sum, square_slots, square_send, square_recv, True)
     for slot in range(SEND_SLOTS):
-        for third in range(3):
+        for third in THIRDS:
             send(6, third, slot).wait_send()
 
     def drain(piece, carry):
-        for third in range(3):
+        for third in THIRDS:
             pair_first(third, piece).wait_send()
         return carry
 
     lax.fori_loop(0, PIECES, drain, 0)
     for unit in range(1, 8):
-        for third in range(3):
+        for third in THIRDS:
             pair_copy(unit, third).wait_send()
     tile_to_everyone(me, lambda owner: square_sum, square_slots, square_send, square_recv, False)
-    total[...] = jnp.full((8, LANES), jnp.sum(square_slots[...]), jnp.float32)
-
-
-def reduce_scatter(grad_attn, grad_mlp, grad_small):
+    total[...] = jnp.full(TILE, jnp.sum(square_slots[...]), jnp.float32)
+
+
+def reduce_scatter(grad_attn, grad_mlp, grad_wide, grad_vec):
     anywhere = pl.BlockSpec(memory_space=pl.ANY)
     inside = pl.BlockSpec(memory_space=pltpu.VMEM)
     dma = pltpu.SemaphoreType.DMA
@@ -239,20 +347,28 @@
         out_shape=(
             pltpu.VMEM((ROWS, LANES), jnp.float32),
             pltpu.VMEM((SMALL_ROWS, LANES), jnp.float32),
-            pltpu.VMEM((8, LANES), jnp.float32),
-            pltpu.HBM((8, 3, THIRD, LANES), jnp.bfloat16),
-            pltpu.HBM((7, 3, THIRD, LANES), jnp.float32),
+            pltpu.VMEM(TILE, jnp.float32),
+            pltpu.HBM((7, 3, THIRD, LANES), jnp.bfloat16),
+            pltpu.HBM((6, 3, THIRD, LANES), jnp.float32),
         ),
-        in_specs=[anywhere] * 3,
+        in_specs=[anywhere] * 4,
         out_specs=(inside, inside, inside, anywhere, anywhere),
         scratch_shapes=[
             pltpu.VMEM((LOAD_SLOTS, 3, PIECE, LANES), jnp.bfloat16),
             pltpu.VMEM((LOAD_SLOTS, 3, PIECE, LANES), jnp.bfloat16),
             pltpu.VMEM((LOAD_SLOTS, 3, 3, PIECE, LANES), jnp.float32),
             pltpu.VMEM((SEND_SLOTS, 3, PIECE, LANES), jnp.float32),
-            pltpu.VMEM((8, LANES), jnp.float32),
+            pltpu.VMEM(TILE, jnp.float32),
             pltpu.VMEM((GROUP, SMALL_ROWS, LANES), jnp.bfloat16),
             pltpu.VMEM((GROUP, 8, LANES), jnp.float32),
+            pltpu.VMEM((3, THIRD, LANES), jnp.bfloat16),
+            pltpu.VMEM((3, THIRD, LANES), jnp.float32),
+            pltpu.VMEM((1, 5120), jnp.bfloat16),
+            pltpu.VMEM((11, 1280), jnp.bfloat16),
+            pltpu.VMEM((8, 5120), jnp.float32),
+            pltpu.VMEM((SMALL_ROWS, 1280), jnp.float32),
+            pltpu.VMEM((GROUP, SMALL_ROWS, LANES), jnp.float32),
+            pltpu.VMEM((GROUP, SMALL_ROWS, LANES), jnp.bfloat16),
             dma((LOAD_SLOTS, 3, 5)),
             dma((SEND_SLOTS, 3)),
             dma((3, PIECES)),
@@ -264,10 +380,10 @@
             dma((GROUP,)),
             dma((GROUP,)),
             dma((GROUP,)),
-            dma(()),
+            dma((2,)),
         ],
         compiler_params=pltpu.CompilerParams(collective_id=0, has_side_effects=True, vmem_limit_bytes=SCATTER_VMEM),
-    )(*[pltpu.with_memory_space_constraint(grad, pltpu.HBM) for grad in (grad_attn, grad_mlp)], grad_small)[:3]
+    )(*[pltpu.with_memory_space_constraint(grad, pltpu.HBM) for grad in (grad_attn, grad_mlp, grad_wide, grad_vec)])[:3]
 
 
 def bank_part(third, attn, mlp):
@@ -275,10 +391,10 @@
 
 
 def update_kernel(sums, small_sums, total, weight_attn, weight_mlp, first_attn, first_mlp, second_attn, second_mlp,
-                  small_weight, small_first, small_second,
-                  update, small_update, part_sums, new_first_attn, new_first_mlp, new_second_attn, new_second_mlp,
-                  small_new_first, small_new_second,
-                  first_out, second_out, out_sems):
+                  weight_wide, weight_vec, first_wide, first_vec, second_wide, second_vec,
+                  update, small_update, small_weight, part_sums, new_first_attn, new_first_mlp, new_second_attn, new_second_mlp,
+                  new_first_wide, new_first_vec, new_second_wide, new_second_vec,
+                  first_out, second_out, small_first, small_second, out_sems):
     clip_coef = jnp.minimum(1.0, MAX_NORM / jnp.sqrt(total[0:1, :]))
 
     def direction(mean_grad, weight, first, second):
@@ -302,7 +418,7 @@
         )
 
     totals = []
-    for third in range(3):
+    for third in THIRDS:
         weight, base = bank_part(third, weight_attn, weight_mlp)
         first, _ = bank_part(third, first_attn, first_mlp)
         second, _ = bank_part(third, second_attn, second_mlp)
@@ -333,19 +449,24 @@
                 copy.start()
             return carry
 
-        zero = jnp.zeros((8, LANES), jnp.float32)
+        zero = jnp.zeros(TILE, jnp.float32)
         totals.append(lax.fori_loop(0, CHUNKS, work, (zero, zero)))
+    pack_rows(weight_wide, weight_vec, small_weight)
+    pack_rows(first_wide, first_vec, small_first)
+    pack_rows(second_wide, second_vec, small_second)
     small, small_m, small_v = direction(small_sums[...], small_weight[...], small_first[...], small_second[...])
     small_update[...] = small
-    small_new_first[...] = small_m
-    small_new_second[...] = small_v
+    small_first[...] = small_m
+    small_second[...] = small_v
+    unpack_rows(small_first, new_first_wide, new_first_vec)
+    unpack_rows(small_second, new_second_wide, new_second_vec)
     old = small_weight[...]
     columns = [
         totals[0][0], totals[0][1], totals[1][0] + totals[2][0], totals[1][1] + totals[2][1],
         (old * old)[0:8], (small * small)[0:8], (old * old)[8:16], (small * small)[8:16],
     ]
-    lane = lax.broadcasted_iota(jnp.int32, (8, LANES), 1)
-    tile = jnp.zeros((8, LANES), jnp.float32)
+    lane = lax.broadcasted_iota(jnp.int32, TILE, 1)
+    tile = jnp.zeros(TILE, jnp.float32)
     for place, column in enumerate(columns):
         tile = jnp.where(lane == place, jnp.sum(column, axis=1, keepdims=True), tile)
     part_sums[...] = tile
@@ -363,7 +484,8 @@
     inside = pl.BlockSpec(memory_space=pltpu.VMEM)
     attn = pltpu.HBM((ATTN_ROWS, LANES), jnp.float32)
     mlp = pltpu.HBM((MLP_ROWS, LANES), jnp.float32)
-    small = jax.ShapeDtypeStruct((SMALL_ROWS, LANES), jnp.float32)
+    wide = jax.ShapeDtypeStruct((1, 320), jnp.float32)
+    vec = jax.ShapeDtypeStruct((11, 80), jnp.float32)
     operands = [sums, small_sums, total, *weights, *firsts, *seconds]
     return pl.pallas_call(
         update_kernel,
@@ -371,14 +493,17 @@
         out_shape=(
             pltpu.VMEM((ROWS, LANES), jnp.float32),
             pltpu.VMEM((SMALL_ROWS, LANES), jnp.float32),
-            pltpu.VMEM((8, LANES), jnp.float32),
-            attn, mlp, attn, mlp, small, small,
+            pltpu.VMEM((SMALL_ROWS, LANES), jnp.float32),
+            pltpu.VMEM(TILE, jnp.float32),
+            attn, mlp, attn, mlp, wide, vec, wide, vec,
         ),
-        in_specs=[inside] * 12,
-        out_specs=(inside, inside, inside, anywhere, anywhere, anywhere, anywhere, inside, inside),
+        in_specs=[inside] * 15,
+        out_specs=(inside,) * 4 + (anywhere,) * 4 + (inside,) * 4,
         scratch_shapes=[
             pltpu.VMEM((OUT_SLOTS, CHUNK, LANES), jnp.float32),
             pltpu.VMEM((OUT_SLOTS, CHUNK, LANES), jnp.float32),
+            pltpu.VMEM((SMALL_ROWS, LANES), jnp.float32),
+            pltpu.VMEM((SMALL_ROWS, LANES), jnp.float32),
             pltpu.SemaphoreType.DMA((OUT_SLOTS, 2)),
         ],
         compiler_params=pltpu.CompilerParams(vmem_limit_bytes=UPDATE_VMEM),
@@ -386,9 +511,10 @@
 
 
 def gather_kernel(part_sums, weight_attn, weight_mlp, update, small_weight, small_update,
-                  everything, all_small, ratios,
-                  fresh_small, slots,
-                  tile_send, tile_recv, small_send, small_recv, own_send, link_send, link_recv, twin_send, twin_recv):
+                  everything, all_wide, all_vec, ratios,
+                  all_small, fresh_small, slots, wide_flat, pair,
+                  tile_send, tile_recv, small_send, small_recv, link_send, link_recv, twin_send, twin_recv,
+                  last_send, last_recv, last_twin_send, last_twin_recv):
     me = lax.axis_index("data")
     twin = flip(me, CORE)
     meet_everyone(me)
@@ -396,7 +522,7 @@
     tile_to_everyone(me, lambda owner: part_sums, slots, tile_send, tile_recv, True)
     tile_to_everyone(me, lambda owner: part_sums, slots, tile_send, tile_recv, False)
     sums = jnp.sum(slots[...], axis=0)
-    lane = lax.broadcasted_iota(jnp.int32, (8, LANES), 1)
+    lane = lax.broadcasted_iota(jnp.int32, TILE, 1)
 
     def column(place):
         return jnp.sum(jnp.where(lane == place, sums, 0.0), axis=1, keepdims=True)
@@ -413,7 +539,7 @@
         return jnp.where(mine, jnp.sum(jnp.where(mine, value, 0.0), axis=0, keepdims=True), value)
 
     def spread(value):
-        return jnp.broadcast_to(value, (8, LANES))
+        return jnp.broadcast_to(value, TILE)
 
     def ratio(weights, updates):
         safe = jnp.where(updates > 0.0, updates, 1.0)
@@ -432,7 +558,7 @@
         return everything.at[owner, pl.ds(third * THIRD, THIRD)]
 
     def link(third, stage, hops):
-        number = {0: 0, 1: 1, 2: 3}[stage] + {(): 0, (0,): 1, (1,): 2, (0, 1): 3}[hops]
+        number = ARRIVALS.index((stage, hops))
         to = flip(me, ORDERS[third][stage])
         owner = flip_all(me, [ORDERS[third][hop] for hop in hops])
         place = place_of(third, owner)
@@ -441,7 +567,7 @@
             device_id=(to,), device_id_type=MESH)
 
     def landed(third, stage, hops):
-        number = {0: 0, 1: 1, 2: 3}[stage] + {(): 0, (0,): 1, (1,): 2, (0, 1): 3}[hops]
+        number = ARRIVALS.index((stage, hops))
         owner = flip_all(flip(me, ORDERS[third][stage]), [ORDERS[third][hop] for hop in hops])
         place = place_of(third, owner)
         return pltpu.make_async_remote_copy(
@@ -462,7 +588,7 @@
             place, place, twin_send.at[third, number], twin_recv.at[third, number],
             device_id=(twin,), device_id_type=MESH)
 
-    for third in range(3):
+    for third in THIRDS:
         scale = LEARN_RATE * (ratio_attn if third == 0 else ratio_mlp)
         weight, base = bank_part(third, weight_attn, weight_mlp)
 
@@ -476,51 +602,67 @@
         lax.fori_loop(0, PIECES, refresh, 0)
         link(third, 0, ()).start()
     for stage in (1, 2):
-        for third in range(3):
+        for third in THIRDS:
             link(third, stage, ()).start()
-    for third in range(3):
+    for third in THIRDS:
         to_twin(third, 0, ()).start()
     low = small_weight[0:8] - LEARN_RATE * ratio_low * small_update[0:8]
     high = small_weight[8:16] - LEARN_RATE * ratio_high * small_update[8:16]
     fresh_small[...] = jnp.concatenate([low, high], axis=0).astype(jnp.bfloat16)
-    own_small = pltpu.make_async_copy(fresh_small, all_small.at[me], own_send)
-    own_small.start()
+    all_small[me] = fresh_small[...]
     tile_to_everyone(me, lambda owner: fresh_small, all_small, small_send, small_recv, True)
 
-    arrivals = (
-        (0, (), ((1, (0,)), (2, (0,)))),
-        (1, (), ((2, (1,)),)),
-        (2, (), ()),
-        (1, (0,), ((2, (0, 1)),)),
-        (2, (0,), ()),
-        (2, (1,), ()),
-        (2, (0, 1), ()),
-    )
-    number = 1
+    def last_part(third, part, owner, to, send_sem, recv_sem):
+        place = everything.at[owner, pl.ds(third * THIRD + part * LAST, LAST)]
+        return pltpu.make_async_remote_copy(
+            place, place, send_sem.at[third, part], recv_sem.at[third, part], device_id=(to,), device_id_type=MESH)
+
+    def last_link(third, part):
+        owner = flip_all(me, ORDERS[third][:2])
+        return last_part(third, part, owner, flip(me, ORDERS[third][2]), last_send, last_recv)
+
+    def last_landed(third, part):
+        return last_part(third, part, flip_all(me, ORDERS[third]), flip(me, ORDERS[third][2]), last_send, last_recv)
+
+    def last_to_twin(third, part):
+        return last_part(third, part, flip_all(me, ORDERS[third]), twin, last_twin_send, last_twin_recv)
+
+    def last_from_twin(third, part):
+        return last_part(third, part, flip_all(twin, ORDERS[third]), twin, last_twin_send, last_twin_recv)
+
     sent = []
-    for stage, hops, forwards in arrivals:
-        for third in range(3):
+    for number, (stage, hops) in enumerate(ARRIVALS):
+        for third in THIRDS:
             landed(third, stage, hops).wait_recv()
-            for forward in forwards:
-                copy = link(third, *forward)
+            for later in () if hops else range(stage + 1, len(THIRDS)):
+                copy = link(third, later, (stage,))
                 copy.start()
                 sent.append(copy)
-            to_twin(third, number, (stage,) + hops).start()
-        number += 1
-    number = 0
-    for hops in ((),) + tuple((stage,) + hops for stage, hops, _ in arrivals):
-        for third in range(3):
-            copy = from_twin(third, number, hops)
-            copy.wait_recv()
+            if hops and stage == 1:
+                for part in range(PARTS):
+                    last_link(third, part).start()
+            to_twin(third, number + 1, (stage,) + hops).start()
+        if number == 2:
+            tile_to_everyone(me, lambda owner: fresh_small, all_small, small_send, small_recv, False)
+            shares_to(all_small, all_wide, all_vec, wide_flat, pair)
+    for number, hops in enumerate(((),) + tuple((stage,) + hops for stage, hops in ARRIVALS)):
+        for third in THIRDS:
+            from_twin(third, number, hops).wait_recv()
             to_twin(third, number, hops).wait_send()
-        number += 1
-    for third in range(3):
+    for third in THIRDS:
         for stage in range(3):
             link(third, stage, ()).wait_send()
     for copy in sent:
         copy.wait_send()
-    own_small.wait()
-    tile_to_everyone(me, lambda owner: fresh_small, all_small, small_send, small_recv, False)
+    for part in range(PARTS):
+        for third in THIRDS:
+            last_landed(third, part).wait_recv()
+            last_to_twin(third, part).start()
+    for part in range(PARTS):
+        for third in THIRDS:
+            last_link(third, part).wait_send()
+            last_to_twin(third, part).wait_send()
+            last_from_twin(third, part).wait_recv()
 
 
 def all_gather(part_sums, weights, update, small_weight, small_update):
@@ -531,19 +673,23 @@
         name="gather",
         out_shape=(
             pltpu.VMEM((GROUP, ROWS, LANES), jnp.bfloat16),
-            pltpu.VMEM((GROUP, SMALL_ROWS, LANES), jnp.bfloat16),
+            pltpu.VMEM((1, 5120), jnp.bfloat16),
+            pltpu.VMEM((11, 1280), jnp.bfloat16),
             pltpu.VMEM((4, 8, LANES), jnp.float32),
         ),
         in_specs=[inside] * 6,
-        out_specs=(inside,) * 3,
+        out_specs=(inside,) * 4,
         scratch_shapes=[
+            pltpu.VMEM((GROUP, SMALL_ROWS, LANES), jnp.bfloat16),
             pltpu.VMEM((SMALL_ROWS, LANES), jnp.bfloat16),
             pltpu.VMEM((GROUP, 8, LANES), jnp.float32),
-            dma((GROUP,)), dma((GROUP,)), dma((GROUP,)), dma((GROUP,)),
-            dma(()), dma((3, 7)), dma((3, 7)), dma((3, 8)), dma((3, 8)),
+            pltpu.VMEM((8, 5120), jnp.float32),
+            pltpu.VMEM((2, SMALL_ROWS, LANES), jnp.float32),
+            *[dma((GROUP,))] * 4,
+            *[dma((len(THIRDS), len(ARRIVALS)))] * 2, *[dma((len(THIRDS), len(ARRIVALS) + 1))] * 2, *[dma((len(THIRDS), PARTS))] * 4,
         ],
         compiler_params=pltpu.CompilerParams(collective_id=1, has_side_effects=True, vmem_limit_bytes=GATHER_VMEM),
-    )(*[resident(value) for value in (part_sums, *weights, update)], small_weight, small_update)
+    )(*[resident(value) for value in (part_sums, *weights, update, small_weight, small_update)])
 
 
 def write_kernel(everything, replica_attn, replica_mlp, attn_sems, mlp_sems):
@@ -576,23 +722,21 @@
     )(resident(everything))
 
 
-def finish_kernel(weight_attn, weight_mlp, update, ratios, all_small, small_weight, small_update,
-                  new_attn, new_mlp, replica_small, new_small,
-                  fresh, fresh_small, weight_sems, small_sems):
-    writes = []
+def finish_kernel(weight_attn, weight_mlp, update, ratios, all_wide, all_vec, small_weight, small_update,
+                  new_attn, new_mlp, replica_wide, replica_vec, new_wide, new_vec,
+                  fresh, fresh_small, weight_sems):
     for tile in range(2):
         rows = pl.ds(8 * tile, 8)
         fresh_small[rows] = small_weight[rows] - LEARN_RATE * ratios[2 + tile] * small_update[rows]
-    for place, (source, to) in enumerate(((all_small, replica_small), (fresh_small, new_small))):
-        copy = pltpu.make_async_copy(source, to, small_sems.at[place])
-        copy.start()
-        writes.append(copy)
+    unpack_rows(fresh_small, new_wide, new_vec)
+    replica_wide[...] = all_wide[...]
+    replica_vec[...] = all_vec[...]
     def write(third, chunk):
         slot = (third * CHUNKS + chunk) % OUT_SLOTS
         to, base = bank_part(third, new_attn, new_mlp)
         return pltpu.make_async_copy(fresh.at[slot], to.at[pl.ds(base + chunk * CHUNK, CHUNK)], weight_sems.at[slot])
 
-    for third in range(3):
+    for third in THIRDS:
         scale = LEARN_RATE * ratios[0 if third == 0 else 1]
         weight, base = bank_part(third, weight_attn, weight_mlp)
 
@@ -617,11 +761,9 @@
         lax.fori_loop(0, CHUNKS, work, 0)
     for place in range(3 * CHUNKS - OUT_SLOTS, 3 * CHUNKS):
         write(place // CHUNKS, place % CHUNKS).wait()
-    for copy in writes:
-        copy.wait()
-
-
-def finish(all_small, weights, update, small_weight, small_update, ratios):
+
+
+def finish(all_wide, all_vec, weights, update, small_weight, small_update, ratios):
     anywhere = pl.BlockSpec(memory_space=pl.ANY)
     inside = pl.BlockSpec(memory_space=pltpu.VMEM)
     dma = pltpu.SemaphoreType.DMA
@@ -631,17 +773,19 @@
         out_shape=(
             pltpu.HBM((ATTN_ROWS, LANES), jnp.float32),
             pltpu.HBM((MLP_ROWS, LANES), jnp.float32),
-            pltpu.HBM((GROUP, SMALL_ROWS, LANES), jnp.bfloat16),
-            pltpu.HBM((SMALL_ROWS, LANES), jnp.float32),
+            jax.ShapeDtypeStruct((1, 5120), jnp.bfloat16),
+            jax.ShapeDtypeStruct((11, 1280), jnp.bfloat16),
+            jax.ShapeDtypeStruct((1, 320), jnp.float32),
+            jax.ShapeDtypeStruct((11, 80), jnp.float32),
         ),
-        in_specs=[inside] * 7,
-        out_specs=(anywhere,) * 4,
+        in_specs=[inside] * 8,
+        out_specs=(anywhere,) * 2 + (inside,) * 4,
         scratch_shapes=[
             pltpu.VMEM((OUT_SLOTS, CHUNK, LANES), jnp.float32), pltpu.VMEM((SMALL_ROWS, LANES), jnp.float32),
-            dma((OUT_SLOTS,)), dma((2,)),
+            dma((OUT_SLOTS,)),
         ],
         compiler_params=pltpu.CompilerParams(vmem_limit_bytes=FINISH_VMEM),
-    )(*[resident(value) for value in (*weights, update, ratios, all_small)], small_weight, small_update)
+    )(*[resident(value) for value in (*weights, update, ratios, all_wide, all_vec, small_weight, small_update)])
 
 
 def linear(bank):
@@ -652,18 +796,6 @@
 def banked(flat, rows):
     blocks = flat.size // (rows * LANES)
     return flat.reshape(blocks, rows, LANES).transpose(1, 0, 2).reshape(rows, blocks * LANES)
-
-
-def pack_small(wide, vec):
-    lead = [(0, 0)] * (wide.ndim - 1)
-    vec_rows = jnp.pad(vec, lead + [(0, 0), (0, LANES - 80)])
-    wide_rows = jnp.pad(wide, lead + [(0, 64)]).reshape(wide.shape[:-1] + (3, LANES))
-    return jnp.concatenate([vec_rows, jnp.pad(wide_rows, lead + [(0, 2), (0, 0)])], axis=-2)
-
-
-def unpack_small(packed):
-    lead = packed.shape[:-2]
-    return packed[..., 11:14, :].reshape(lead + (3 * LANES,))[..., :320], packed[..., :11, :80]
 
 
 def solution(mesh):
@@ -675,32 +807,20 @@
         grads = banks[0:4]
         attn_grad = linear(grads[0][0]).reshape(GROUP, ATTN_ROWS, LANES)
         mlp_grad = linear(grads[1][0]).reshape(GROUP, MLP_ROWS, LANES)
-        small_grad = pack_small(grads[2][0].reshape(GROUP, 320), grads[3][0].reshape(11, GROUP, 80).transpose(1, 0, 2))
-        states, smalls = [], []
-        for first in (4, 8, 12):
-            attn, mlp, wide, vec = banks[first:first + 4]
-            states.append((linear(attn), linear(mlp)))
-            smalls.append(pack_small(wide[0], vec))
-        small_grad, *smalls = lax.optimization_barrier((small_grad, *smalls))
-        sums, small_sums, total = reduce_scatter(attn_grad, mlp_grad, small_grad)
-        update, small_update, part_sums, *moments = update_step(sums, small_sums, total, *states, smalls)
-        everything, all_small, ratios = all_gather(part_sums, states[0], update, smalls[0], small_update)
+        states = [(linear(banks[first]), linear(banks[first + 1])) for first in (4, 8, 12)]
+        smalls = [bank for first in (4, 8, 12) for bank in banks[first + 2:first + 4]]
+        sums, small_sums, total = reduce_scatter(attn_grad, mlp_grad, grads[2][0], grads[3][0])
+        update, small_update, small_weight, part_sums, *moments = update_step(sums, small_sums, total, *states, smalls)
+        everything, all_wide, all_vec, ratios = all_gather(part_sums, states[0], update, small_weight, small_update)
         replica_attn, replica_mlp = write_replica(everything)
-        replica_attn, all_small = lax.optimization_barrier((replica_attn, all_small))
-        new_attn, new_mlp, all_small, new_small = finish(
-            all_small, states[0], update, smalls[0], small_update, ratios)
-        replica_wide, replica_vec = unpack_small(all_small)
-        outs = [
-            banked(replica_attn, 4), banked(replica_mlp, 2), replica_wide.reshape(1, 5120),
-            replica_vec.transpose(1, 0, 2).reshape(11, 1280),
-        ]
-        for attn, mlp, small in (
-            (new_attn, new_mlp, new_small),
-            (moments[0], moments[1], moments[4]),
-            (moments[2], moments[3], moments[5]),
-        ):
-            wide, vec = unpack_small(small)
-            outs += [banked(attn, 4), banked(mlp, 2), wide[None], vec]
-        return tuple(outs)
+        replica_attn, all_wide = lax.optimization_barrier((replica_attn, all_wide))
+        new_attn, new_mlp, replica_wide, replica_vec, new_wide, new_vec = finish(
+            all_wide, all_vec, states[0], update, small_weight, small_update, ratios)
+        return (
+            banked(replica_attn, 4), banked(replica_mlp, 2), replica_wide, replica_vec,
+            banked(new_attn, 4), banked(new_mlp, 2), new_wide, new_vec,
+            banked(moments[0], 4), banked(moments[1], 2), moments[4], moments[5],
+            banked(moments[2], 4), banked(moments[3], 2), moments[6], moments[7],
+        )
 
     return jax.shard_map(local_step, mesh=mesh, in_specs=(grad_spec,) * 4 + (shard_spec,) * 12, out_specs=(full_spec,) * 4 + (shard_spec,) * 12, check_vma=False)

time: 440 us -> 424 us (0.964)
  local copies, waits for them, and re-layouts: 7.91 us -> 0.05 us
where the time goes in v3:
time: 424 us
  Pallas kernels  423 us (100%)
    pallas_call x1, Pallas kernels, reduce_scatter(): pl.pallas_call(scatter_kernel, name='scatter', out_shape=(pltpu.VMEM((ROW...  263 us
    pallas_call x1, Pallas kernels, all_gather(): pl.pallas_call(gather_kernel, name='gather', out_shape=(pltpu.VMEM((GROUP...  136 us
    pallas_call x1, Pallas kernels, write_replica(): pl.pallas_call(write_kernel, name='write', out_shape=(pltpu.HBM((GROUP *...  12.9 us

profile of v3, /device:TPU:0, one launch (start us, length us, event | category | flops | bytes accessed | tf_op | source)
XLA Modules:
  0.0 424.3 jit_solution(12611667203242508861)
XLA Ops:
  0.7 0.0 copy-start
  0.7 0.0 copy-start.1
  0.7 0.0 copy-start.2
  0.7 0.0 copy-start.3
  0.7 0.0 copy-start.4
  0.7 0.0 copy-start.5
  0.7 0.0 copy-start.6
  0.7 0.0 copy-start.7
  0.7 0.0 copy-start.8
  0.7 0.0 copy-start.9
  0.8 0.0 copy-start.10
  0.8 0.0 copy-start.11
  0.8 263.1 %scatter.1 = (f32[9600,128]{1,0:T(8,128)S(1)}, f32[16,128]{1,0:T(8,128)S(1)}, f32[8,128]{1,0:T(8,128)S(1)}, bf16[7,3,3200,128]{3,2,1,0:T(8,128)(2,1)}, f32[6,3,3200,128]{3,2,1,0:T(8,128)}) custom-call(bf16[16,3200,128]{2,1,0:T(8,128)(2,1)} %bitcast.93, bf16[16,6400,128]{2,1,0:T(8,128)(2,1)} %bitcast.92, bf16[1,5120]{1,0:T(2,128)(2,1)} %bitcast.95, ...), custom_call_target="tpu_custom_call" | custom-call | tf_op jit(solution)/shard_map/scatter/pallas_call | solution.py:344
  263.9 0.0 copy-done
  263.9 0.0 copy-done.1
  263.9 0.0 copy-done.2
  263.9 0.0 copy-done.3
  263.9 0.0 copy-done.4
  263.9 0.0 copy-done.5
  263.9 0.0 copy-done.6
  264.0 0.0 copy-done.7
  264.0 0.0 copy-done.8
  264.0 0.0 copy-done.9
  264.0 0.0 copy-done.10
  264.0 0.0 copy-done.11
  264.0 7.7 %update.1 = (f32[9600,128]{1,0:T(8,128)S(1)}, f32[16,128]{1,0:T(8,128)S(1)}, f32[16,128]{1,0:T(8,128)S(1)}, f32[8,128]{1,0:T(8,128)S(1)}, f32[3200,128]{1,0:T(8,...) custom-call(f32[9600,128]{1,0:T(8,128)S(1)} %get-tuple-element.45.su, ...), custom_call_target="tpu_custom_call" | custom-call | tf_op jit(solution)/shard_map/update/pallas_call | solution.py:490
  271.7 135.5 %gather.1 = (bf16[16,9600,128]{2,1,0:T(8,128)(2,1)S(1)}, bf16[1,5120]{1,0:T(2,128)(2,1)S(1)}, bf16[11,1280]{1,0:T(8,128)(2,1)S(1)}, f32[4,8,128]{2,1,0:T(8,128)S(1)}) custom-call(f32[8,128]{1,0:T(8,128)S(1)} %get-tuple-element.48.part_sums, f32[3200,128]{1,0:T(8,128)S(1)} %bitcast.86, f32[6400,128]{1,0:T(8,128)S(1)} %bitcast.83, ...), custom_call_target="tpu_custom_call" | custom-call | tf_op jit(solution)/shard_map/gather/pallas_call | solution.py:671
  407.3 12.9 %write.1 = (bf16[51200,128]{1,0:T(8,128)(2,1)}, bf16[102400,128]{1,0:T(8,128)(2,1)}) custom-call(bf16[16,9600,128]{2,1,0:T(8,128)(2,1)S(1)} %get-tuple-element.52.everything), custom_call_target="tpu_custom_call" | custom-call | tf_op jit(solution)/shard_map/write/pallas_call | solution.py:711
  420.2 4.1 finish.1
Async XLA Ops:
  0.7 263.2 %copy-start = (f32[2,409600]{1,0:T(2,128)S(1)}, f32[2,409600]{1,0:T(2,128)}, u32[]{:S(2)}) copy-start(f32[2,409600]{1,0:T(2,128)} %param.21) | copy-start | bytes 9830404
  0.7 263.2 %copy-start.1 = (f32[4,102400]{1,0:T(4,128)S(1)}, f32[4,102400]{1,0:T(4,128)}, u32[]{:S(2)}) copy-start(f32[4,102400]{1,0:T(4,128)} %param.20) | copy-start | bytes 4915204
  0.7 263.2 %copy-start.2 = (f32[2,409600]{1,0:T(2,128)S(1)}, f32[2,409600]{1,0:T(2,128)}, u32[]{:S(2)}) copy-start(f32[2,409600]{1,0:T(2,128)} %param.25) | copy-start | bytes 9830404
  0.7 263.2 %copy-start.3 = (f32[2,409600]{1,0:T(2,128)S(1)}, f32[2,409600]{1,0:T(2,128)}, u32[]{:S(2)}) copy-start(f32[2,409600]{1,0:T(2,128)} %param.29) | copy-start | bytes 9830404
  0.7 263.2 %copy-start.4 = (f32[4,102400]{1,0:T(4,128)S(1)}, f32[4,102400]{1,0:T(4,128)}, u32[]{:S(2)}) copy-start(f32[4,102400]{1,0:T(4,128)} %param.24) | copy-start | bytes 4915204
  0.7 263.2 %copy-start.5 = (f32[4,102400]{1,0:T(4,128)S(1)}, f32[4,102400]{1,0:T(4,128)}, u32[]{:S(2)}) copy-start(f32[4,102400]{1,0:T(4,128)} %param.28) | copy-start | bytes 4915204
  0.7 263.2 %copy-start.6 = (f32[11,80]{1,0:T(8,128)S(1)}, f32[11,80]{1,0:T(8,128)}, u32[]{:S(2)}) copy-start(f32[11,80]{1,0:T(8,128)} %weight_vec.1) | copy-start | bytes 10564
  0.7 263.2 %copy-start.7 = (f32[11,80]{1,0:T(8,128)S(1)}, f32[11,80]{1,0:T(8,128)}, u32[]{:S(2)}) copy-start(f32[11,80]{1,0:T(8,128)} %first_vec.1) | copy-start | bytes 10564
  0.7 263.2 %copy-start.8 = (f32[11,80]{1,0:T(8,128)S(1)}, f32[11,80]{1,0:T(8,128)}, u32[]{:S(2)}) copy-start(f32[11,80]{1,0:T(8,128)} %second_vec.1) | copy-start | bytes 10564
  0.7 263.2 %copy-start.9 = (f32[1,320]{1,0:T(1,128)S(1)}, f32[1,320]{1,0:T(1,128)}, u32[]{:S(2)}) copy-start(f32[1,320]{1,0:T(1,128)} %weight_wide.1) | copy-start | bytes 3844
  0.8 263.2 %copy-start.10 = (f32[1,320]{1,0:T(1,128)S(1)}, f32[1,320]{1,0:T(1,128)}, u32[]{:S(2)}) copy-start(f32[1,320]{1,0:T(1,128)} %first_wide.1) | copy-start | bytes 3844
  0.8 263.2 %copy-start.11 = (f32[1,320]{1,0:T(1,128)S(1)}, f32[1,320]{1,0:T(1,128)}, u32[]{:S(2)}) copy-start(f32[1,320]{1,0:T(1,128)} %second_wide.1) | copy-start | bytes 3844

commit v4 on v3

--- a/solution.py
+++ b/solution.py
@@ -14,6 +14,7 @@
 EPSILON = 1e-6
 WEIGHT_DECAY = 0.01
 MAX_NORM = 1.0
+ROOT_FLOOR = 1e-36
 
 MESH = pl.DeviceIdType.MESH
 GROUP = 16
@@ -36,9 +37,10 @@
 LOAD_SLOTS = 3
 SEND_SLOTS = 4
 SMALL_ROWS = 16
-BLOCK = 64
+BLOCK = 320
 PARTS = 4
 LAST = THIRD // PARTS
+OWN_PARTS = ((0, 640), (640, 2560))
 CHUNK = 640
 CHUNKS = THIRD // CHUNK
 OUT_SLOTS = 4
@@ -73,7 +75,7 @@
     return index
 
 
-def meet_everyone(me):
+def greet_everyone(me):
     barrier = pltpu.get_barrier_semaphore()
 
     def signal(step, carry):
@@ -81,7 +83,10 @@
         return carry
 
     lax.fori_loop(1, GROUP, signal, 0)
-    pl.semaphore_wait(barrier, GROUP - 1)
+
+
+def meet_everyone():
+    pl.semaphore_wait(pltpu.get_barrier_semaphore(), GROUP - 1)
 
 
 def tile_to_everyone(me, source_of, slots, send_sems, recv_sems, begin):
@@ -185,7 +190,7 @@
                    small_send, small_recv, square_send, square_recv, local_sems):
     me = lax.axis_index("data")
     twin = flip(me, CORE)
-    meet_everyone(me)
+    greet_everyone(me)
 
     def grad_of(third, owner, row, count):
         if third == 0:
@@ -211,12 +216,10 @@
             pair_first(third, piece).start()
         return carry
 
-    lax.fori_loop(0, PIECES, start_first, 0)
     own_small = (
         pltpu.make_async_copy(grad_wide, wide_raw, local_sems.at[0]), pltpu.make_async_copy(grad_vec, vec_raw, local_sems.at[1]))
     for copy in own_small:
         copy.start()
-    square_sum[...] = jnp.zeros_like(square_sum)
 
     def loads(unit, third, piece):
         rows = piece * PIECE
@@ -255,6 +258,8 @@
     ahead = LOAD_SLOTS - 1
     for piece in range(ahead):
         begin(0, piece)
+    meet_everyone()
+    lax.fori_loop(0, PIECES, start_first, 0)
 
     for unit in range(8):
         def work(piece, carry, unit=unit):
@@ -312,13 +317,13 @@
             small_slots[me] = small_shares[me]
         if unit == 1:
             tile_to_everyone(me, lambda owner: small_shares.at[owner], small_slots, small_send, small_recv, True)
-
-    tile_to_everyone(me, lambda owner: small_shares.at[owner], small_slots, small_send, small_recv, False)
-    small = jnp.sum(small_slots[...].astype(jnp.float32), axis=0) * (1.0 / GROUP)
-    small_sums[...] = small
-    squares = square_sum[...] + (small * small)[0:8] + (small * small)[8:16]
-    square_sum[...] = squares
-    square_slots[me] = squares
+        if unit == 5:
+            tile_to_everyone(me, lambda owner: small_shares.at[owner], small_slots, small_send, small_recv, False)
+            small = jnp.sum(small_slots[...].astype(jnp.float32), axis=0) * (1.0 / GROUP)
+            small_sums[...] = small
+            square_sum[...] = (small * small)[0:8] + (small * small)[8:16]
+
+    square_slots[me] = square_sum[...]
     tile_to_everyone(me, lambda owner: square_sum, square_slots, square_send, square_recv, True)
     for slot in range(SEND_SLOTS):
         for third in THIRDS:
@@ -397,12 +402,17 @@
                   first_out, second_out, small_first, small_second, out_sems):
     clip_coef = jnp.minimum(1.0, MAX_NORM / jnp.sqrt(total[0:1, :]))
 
+    first_step = (1.0 - BETA_FIRST) * clip_coef
+    second_step = (1.0 - BETA_SECOND) * clip_coef * clip_coef
+    first_bias = 1.0 - BETA_FIRST ** STEP_NUMBER
+    root_scale = first_bias ** 2 / (1.0 - BETA_SECOND ** STEP_NUMBER)
+
     def direction(mean_grad, weight, first, second):
-        clipped = clip_coef * mean_grad
-        new_first = BETA_FIRST * first + (1.0 - BETA_FIRST) * clipped
-        new_second = BETA_SECOND * second + (1.0 - BETA_SECOND) * (clipped * clipped)
-        root = jnp.sqrt(new_second * (1.0 / (1.0 - BETA_SECOND ** STEP_NUMBER))) + EPSILON
-        return (new_first * (1.0 / (1.0 - BETA_FIRST ** STEP_NUMBER))) / root + WEIGHT_DECAY * weight, new_first, new_second
+        new_first = BETA_FIRST * first + first_step * mean_grad
+        new_second = BETA_SECOND * second + second_step * (mean_grad * mean_grad)
+        square = jnp.maximum(new_second * root_scale, ROOT_FLOOR)
+        root = square * lax.rsqrt(square) + EPSILON * first_bias
+        return new_first / root + WEIGHT_DECAY * weight, new_first, new_second
 
     def tile_sum(value):
         return jnp.sum((value * value).reshape(-1, 8, LANES), axis=0)
@@ -511,13 +521,14 @@
 
 
 def gather_kernel(part_sums, weight_attn, weight_mlp, update, small_weight, small_update,
-                  everything, all_wide, all_vec, ratios,
-                  all_small, fresh_small, slots, wide_flat, pair,
+                  everything, all_wide, all_vec, new_weight, new_wide, new_vec,
+                  all_small, fresh_small, new_small, slots, wide_flat, pair,
                   tile_send, tile_recv, small_send, small_recv, link_send, link_recv, twin_send, twin_recv,
-                  last_send, last_recv, last_twin_send, last_twin_recv):
+                  own_send, own_recv, last_send, last_recv, last_twin_send, last_twin_recv):
     me = lax.axis_index("data")
     twin = flip(me, CORE)
-    meet_everyone(me)
+    greet_everyone(me)
+    meet_everyone()
     slots[me] = part_sums[...]
     tile_to_everyone(me, lambda owner: part_sums, slots, tile_send, tile_recv, True)
     tile_to_everyone(me, lambda owner: part_sums, slots, tile_send, tile_recv, False)
@@ -549,10 +560,6 @@
     ratio_mlp = ratio(same_tensor(spread(column(2)), 2), same_tensor(spread(column(3)), 2))
     ratio_low = ratio(spread(column(4)), spread(column(5)))
     ratio_high = ratio(spread(wide_rows(column(6))), spread(wide_rows(column(7))))
-    ratios[0] = ratio_attn
-    ratios[1] = ratio_mlp
-    ratios[2] = ratio_low
-    ratios[3] = ratio_high
 
     def place_of(third, owner):
         return everything.at[owner, pl.ds(third * THIRD, THIRD)]
@@ -588,19 +595,29 @@
             place, place, twin_send.at[third, number], twin_recv.at[third, number],
             device_id=(twin,), device_id_type=MESH)
 
-    for third in THIRDS:
-        scale = LEARN_RATE * (ratio_attn if third == 0 else ratio_mlp)
-        weight, base = bank_part(third, weight_attn, weight_mlp)
-
-        def refresh(piece, carry, third=third, scale=scale, weight=weight, base=base):
-            rows = pl.ds(pl.multiple_of(third * THIRD + piece * PIECE, PIECE), PIECE)
-            old = weight[pl.ds(pl.multiple_of(base + piece * PIECE, PIECE), PIECE)].reshape(PIECE // 8, 8, LANES)
-            step = update[rows].reshape(PIECE // 8, 8, LANES)
-            everything[me, rows] = (old - scale[None] * step).reshape(PIECE, LANES).astype(jnp.bfloat16)
-            return carry
-
-        lax.fori_loop(0, PIECES, refresh, 0)
-        link(third, 0, ()).start()
+    def own_part(third, part, owner):
+        start, rows = OWN_PARTS[part]
+        place = everything.at[owner, pl.ds(third * THIRD + start, rows)]
+        return pltpu.make_async_remote_copy(
+            place, place, own_send.at[third, part], own_recv.at[third, part],
+            device_id=(flip(me, ORDERS[third][0]),), device_id_type=MESH)
+
+    for part, (first_row, rows_here) in enumerate(OWN_PARTS):
+        for third in THIRDS:
+            scale = LEARN_RATE * (ratio_attn if third == 0 else ratio_mlp)
+            weight, base = bank_part(third, weight_attn, weight_mlp)
+
+            def refresh(piece, carry, third=third, scale=scale, weight=weight, base=base, first_row=first_row):
+                row = first_row + piece * BLOCK
+                rows = pl.ds(pl.multiple_of(third * THIRD + row, BLOCK), BLOCK)
+                old = weight[pl.ds(pl.multiple_of(base + row, BLOCK), BLOCK)].reshape((-1,) + TILE)
+                new = (old - scale[None] * update[rows].reshape((-1,) + TILE)).reshape(BLOCK, LANES)
+                new_weight[rows] = new
+                everything[me, rows] = new.astype(jnp.bfloat16)
+                return carry
+
+            lax.fori_loop(0, rows_here // BLOCK, refresh, 0)
+            own_part(third, part, me).start()
     for stage in (1, 2):
         for third in THIRDS:
             link(third, stage, ()).start()
@@ -608,7 +625,9 @@
         to_twin(third, 0, ()).start()
     low = small_weight[0:8] - LEARN_RATE * ratio_low * small_update[0:8]
     high = small_weight[8:16] - LEARN_RATE * ratio_high * small_update[8:16]
-    fresh_small[...] = jnp.concatenate([low, high], axis=0).astype(jnp.bfloat16)
+    new_small[...] = jnp.concatenate([low, high], axis=0)
+    unpack_rows(new_small, new_wide, new_vec)
+    fresh_small[...] = new_small[...].astype(jnp.bfloat16)
     all_small[me] = fresh_small[...]
     tile_to_everyone(me, lambda owner: fresh_small, all_small, small_send, small_recv, True)
 
@@ -633,7 +652,11 @@
     sent = []
     for number, (stage, hops) in enumerate(ARRIVALS):
         for third in THIRDS:
-            landed(third, stage, hops).wait_recv()
+            if number == 0:
+                for part in range(len(OWN_PARTS)):
+                    own_part(third, part, flip(me, ORDERS[third][0])).wait_recv()
+            else:
+                landed(third, stage, hops).wait_recv()
             for later in () if hops else range(stage + 1, len(THIRDS)):
                 copy = link(third, later, (stage,))
                 copy.start()
@@ -650,7 +673,9 @@
             from_twin(third, number, hops).wait_recv()
             to_twin(third, number, hops).wait_send()
     for third in THIRDS:
-        for stage in range(3):
+        for part in range(len(OWN_PARTS)):
+            own_part(third, part, me).wait_send()
+        for stage in (1, 2):
             link(third, stage, ()).wait_send()
     for copy in sent:
         copy.wait_send()
@@ -673,20 +698,23 @@
         name="gather",
         out_shape=(
             pltpu.VMEM((GROUP, ROWS, LANES), jnp.bfloat16),
-            pltpu.VMEM((1, 5120), jnp.bfloat16),
-            pltpu.VMEM((11, 1280), jnp.bfloat16),
-            pltpu.VMEM((4, 8, LANES), jnp.float32),
+            pltpu.VMEM((1, WIDE), jnp.bfloat16),
+            pltpu.VMEM((VECS, VEC), jnp.bfloat16),
+            pltpu.VMEM((ROWS, LANES), jnp.float32),
+            pltpu.VMEM((1, WIDE_SHARE), jnp.float32),
+            pltpu.VMEM((VECS, VEC_SHARE), jnp.float32),
         ),
         in_specs=[inside] * 6,
-        out_specs=(inside,) * 4,
+        out_specs=(inside,) * 6,
         scratch_shapes=[
             pltpu.VMEM((GROUP, SMALL_ROWS, LANES), jnp.bfloat16),
             pltpu.VMEM((SMALL_ROWS, LANES), jnp.bfloat16),
+            pltpu.VMEM((SMALL_ROWS, LANES), jnp.float32),
             pltpu.VMEM((GROUP, 8, LANES), jnp.float32),
             pltpu.VMEM((8, 5120), jnp.float32),
             pltpu.VMEM((2, SMALL_ROWS, LANES), jnp.float32),
             *[dma((GROUP,))] * 4,
-            *[dma((len(THIRDS), len(ARRIVALS)))] * 2, *[dma((len(THIRDS), len(ARRIVALS) + 1))] * 2, *[dma((len(THIRDS), PARTS))] * 4,
+            *[dma((len(THIRDS), len(ARRIVALS)))] * 2, *[dma((len(THIRDS), len(ARRIVALS) + 1))] * 2, *[dma((len(THIRDS), len(OWN_PARTS)))] * 2, *[dma((len(THIRDS), PARTS))] * 4,
         ],
         compiler_params=pltpu.CompilerParams(collective_id=1, has_side_effects=True, vmem_limit_bytes=GATHER_VMEM),
     )(*[resident(value) for value in (part_sums, *weights, update, small_weight, small_update)])
@@ -722,70 +750,38 @@
     )(resident(everything))
 
 
-def finish_kernel(weight_attn, weight_mlp, update, ratios, all_wide, all_vec, small_weight, small_update,
-                  new_attn, new_mlp, replica_wide, replica_vec, new_wide, new_vec,
-                  fresh, fresh_small, weight_sems):
-    for tile in range(2):
-        rows = pl.ds(8 * tile, 8)
-        fresh_small[rows] = small_weight[rows] - LEARN_RATE * ratios[2 + tile] * small_update[rows]
-    unpack_rows(fresh_small, new_wide, new_vec)
-    replica_wide[...] = all_wide[...]
-    replica_vec[...] = all_vec[...]
-    def write(third, chunk):
-        slot = (third * CHUNKS + chunk) % OUT_SLOTS
-        to, base = bank_part(third, new_attn, new_mlp)
-        return pltpu.make_async_copy(fresh.at[slot], to.at[pl.ds(base + chunk * CHUNK, CHUNK)], weight_sems.at[slot])
-
-    for third in THIRDS:
-        scale = LEARN_RATE * ratios[0 if third == 0 else 1]
-        weight, base = bank_part(third, weight_attn, weight_mlp)
-
-        def work(chunk, carry, third=third, scale=scale, weight=weight, base=base):
-            slot = (third * CHUNKS + chunk) % OUT_SLOTS
-
-            @pl.when(third * CHUNKS + chunk >= OUT_SLOTS)
-            def _():
-                write(third, chunk).wait()
-
-            def refresh(block, inner):
-                start = chunk * CHUNK + block * BLOCK
-                old = weight[pl.ds(pl.multiple_of(base + start, BLOCK), BLOCK)].reshape(BLOCK // 8, 8, LANES)
-                step = update[pl.ds(pl.multiple_of(third * THIRD + start, BLOCK), BLOCK)].reshape(BLOCK // 8, 8, LANES)
-                fresh[slot, pl.ds(pl.multiple_of(block * BLOCK, BLOCK), BLOCK)] = (old - scale[None] * step).reshape(BLOCK, LANES)
-                return inner
-
-            lax.fori_loop(0, CHUNK // BLOCK, refresh, 0)
-            write(third, chunk).start()
-            return carry
-
-        lax.fori_loop(0, CHUNKS, work, 0)
-    for place in range(3 * CHUNKS - OUT_SLOTS, 3 * CHUNKS):
-        write(place // CHUNKS, place % CHUNKS).wait()
-
-
-def finish(all_wide, all_vec, weights, update, small_weight, small_update, ratios):
+def finish_kernel(new_weight, wide_in, vec_in, all_wide, all_vec, new_attn, new_mlp, new_wide, new_vec, replica_wide, replica_vec, sems):
+    copies = [
+        pltpu.make_async_copy(new_weight.at[pl.ds(0, ATTN_ROWS)], new_attn, sems.at[0]),
+        pltpu.make_async_copy(new_weight.at[pl.ds(ATTN_ROWS, MLP_ROWS)], new_mlp, sems.at[1]),
+    ]
+    for number, (source, to) in enumerate(((wide_in, new_wide), (vec_in, new_vec), (all_wide, replica_wide), (all_vec, replica_vec))):
+        copies.append(pltpu.make_async_copy(source, to, sems.at[number + 2]))
+    for copy in copies:
+        copy.start()
+    for copy in copies:
+        copy.wait()
+
+
+def finish(new_weight, new_wide, new_vec, all_wide, all_vec):
     anywhere = pl.BlockSpec(memory_space=pl.ANY)
     inside = pl.BlockSpec(memory_space=pltpu.VMEM)
-    dma = pltpu.SemaphoreType.DMA
     return pl.pallas_call(
         finish_kernel,
         name="finish",
         out_shape=(
             pltpu.HBM((ATTN_ROWS, LANES), jnp.float32),
             pltpu.HBM((MLP_ROWS, LANES), jnp.float32),
-            jax.ShapeDtypeStruct((1, 5120), jnp.bfloat16),
-            jax.ShapeDtypeStruct((11, 1280), jnp.bfloat16),
-            jax.ShapeDtypeStruct((1, 320), jnp.float32),
-            jax.ShapeDtypeStruct((11, 80), jnp.float32),
+            pltpu.HBM(new_wide.shape, jnp.float32),
+            pltpu.HBM(new_vec.shape, jnp.float32),
+            pltpu.HBM(all_wide.shape, jnp.bfloat16),
+            pltpu.HBM(all_vec.shape, jnp.bfloat16),
         ),
-        in_specs=[inside] * 8,
-        out_specs=(anywhere,) * 2 + (inside,) * 4,
-        scratch_shapes=[
-            pltpu.VMEM((OUT_SLOTS, CHUNK, LANES), jnp.float32), pltpu.VMEM((SMALL_ROWS, LANES), jnp.float32),
-            dma((OUT_SLOTS,)),
-        ],
+        in_specs=[inside] * 5,
+        out_specs=(anywhere,) * 6,
+        scratch_shapes=[pltpu.SemaphoreType.DMA((6,))],
         compiler_params=pltpu.CompilerParams(vmem_limit_bytes=FINISH_VMEM),
-    )(*[resident(value) for value in (*weights, update, ratios, all_wide, all_vec, small_weight, small_update)])
+    )(*[resident(value) for value in (new_weight, new_wide, new_vec, all_wide, all_vec)])
 
 
 def linear(bank):
@@ -811,11 +807,10 @@
         smalls = [bank for first in (4, 8, 12) for bank in banks[first + 2:first + 4]]
         sums, small_sums, total = reduce_scatter(attn_grad, mlp_grad, grads[2][0], grads[3][0])
         update, small_update, small_weight, part_sums, *moments = update_step(sums, small_sums, total, *states, smalls)
-        everything, all_wide, all_vec, ratios = all_gather(part_sums, states[0], update, small_weight, small_update)
+        everything, all_wide, all_vec, *new = all_gather(part_sums, states[0], update, small_weight, small_update)
         replica_attn, replica_mlp = write_replica(everything)
         replica_attn, all_wide = lax.optimization_barrier((replica_attn, all_wide))
-        new_attn, new_mlp, replica_wide, replica_vec, new_wide, new_vec = finish(
-            all_wide, all_vec, states[0], update, small_weight, small_update, ratios)
+        new_attn, new_mlp, new_wide, new_vec, replica_wide, replica_vec = finish(*new, all_wide, all_vec)
         return (
             banked(replica_attn, 4), banked(replica_mlp, 2), replica_wide, replica_vec,
             banked(new_attn, 4), banked(new_mlp, 2), new_wide, new_vec,

time: 424 us -> 419 us (0.988)
  Pallas kernels: 423 us -> 418 us
where the time goes in v4:
time: 419 us
  Pallas kernels  418 us (100%)
    pallas_call x1, Pallas kernels, reduce_scatter(): pl.pallas_call(scatter_kernel, name='scatter', out_shape=(pltpu.VMEM((ROW...  262 us
    pallas_call x1, Pallas kernels, all_gather(): pl.pallas_call(gather_kernel, name='gather', out_shape=(pltpu.VMEM((GROUP...  135 us
    pallas_call x1, Pallas kernels, write_replica(): pl.pallas_call(write_kernel, name='write', out_shape=(pltpu.HBM((GROUP *...  12.9 us

profile of v4, /device:TPU:0, one launch (start us, length us, event | category | flops | bytes accessed | tf_op | source)
XLA Modules:
  0.0 419.0 jit_solution(12658769012738292108)
XLA Ops:
  0.7 0.0 copy-start
  0.7 0.0 copy-start.1
  0.7 0.0 copy-start.2
  0.7 0.0 copy-start.3
  0.7 0.0 copy-start.4
  0.7 0.0 copy-start.5
  0.7 0.0 copy-start.6
  0.7 0.0 copy-start.7
  0.7 0.0 copy-start.8
  0.7 0.0 copy-start.9
  0.8 0.0 copy-start.10
  0.8 0.0 copy-start.11
  0.8 262.3 %scatter.1 = (f32[9600,128]{1,0:T(8,128)S(1)}, f32[16,128]{1,0:T(8,128)S(1)}, f32[8,128]{1,0:T(8,128)S(1)}, bf16[7,3,3200,128]{3,2,1,0:T(8,128)(2,1)}, f32[6,3,3200,128]{3,2,1,0:T(8,128)}) custom-call(bf16[16,3200,128]{2,1,0:T(8,128)(2,1)} %bitcast.91, bf16[16,6400,128]{2,1,0:T(8,128)(2,1)} %bitcast.90, bf16[1,5120]{1,0:T(2,128)(2,1)} %bitcast.93, ...), custom_call_target="tpu_custom_call" | custom-call | tf_op jit(solution)/shard_map/scatter/pallas_call | solution.py:349
  263.1 0.0 copy-done
  263.1 0.0 copy-done.1
  263.1 0.0 copy-done.2
  263.1 0.0 copy-done.3
  263.1 0.0 copy-done.4
  263.1 0.0 copy-done.5
  263.1 0.0 copy-done.6
  263.1 0.0 copy-done.7
  263.1 0.0 copy-done.8
  263.2 0.0 copy-done.9
  263.2 0.0 copy-done.10
  263.2 0.0 copy-done.11
  263.2 5.5 %update.1 = (f32[9600,128]{1,0:T(8,128)S(1)}, f32[16,128]{1,0:T(8,128)S(1)}, f32[16,128]{1,0:T(8,128)S(1)}, f32[8,128]{1,0:T(8,128)S(1)}, f32[3200,128]{1,0:T(8,...) custom-call(f32[9600,128]{1,0:T(8,128)S(1)} %get-tuple-element.47.su, ...), custom_call_target="tpu_custom_call" | custom-call | tf_op jit(solution)/shard_map/update/pallas_call | solution.py:500
  268.7 135.0 %gather.1 = (bf16[16,9600,128]{2,1,0:T(8,128)(2,1)S(1)}, bf16[1,5120]{1,0:T(2,128)(2,1)S(1)}, bf16[11,1280]{1,0:T(8,128)(2,1)S(1)}, f32[9600,128]{1,0:T(8,128)S(...) custom-call(f32[8,128]{1,0:T(8,128)S(1)} %get-tuple-element.50.part_sums, f32[3200,128]{1,0:T(8,128)S(1)} %bitcast.85, ...), custom_call_target="tpu_custom_call" | custom-call | tf_op jit(solution)/shard_map/gather/pallas_call | solution.py:696
  403.7 12.9 %write.1 = (bf16[51200,128]{1,0:T(8,128)(2,1)}, bf16[102400,128]{1,0:T(8,128)(2,1)}) custom-call(bf16[16,9600,128]{2,1,0:T(8,128)(2,1)S(1)} %get-tuple-element.54.everything), custom_call_target="tpu_custom_call" | custom-call | tf_op jit(solution)/shard_map/write/pallas_call | solution.py:739
  416.7 2.3 finish.1
Async XLA Ops:
  0.7 262.4 %copy-start = (f32[2,409600]{1,0:T(2,128)S(1)}, f32[2,409600]{1,0:T(2,128)}, u32[]{:S(2)}) copy-start(f32[2,409600]{1,0:T(2,128)} %param.21) | copy-start | bytes 9830404
  0.7 262.4 %copy-start.1 = (f32[4,102400]{1,0:T(4,128)S(1)}, f32[4,102400]{1,0:T(4,128)}, u32[]{:S(2)}) copy-start(f32[4,102400]{1,0:T(4,128)} %param.20) | copy-start | bytes 4915204
  0.7 262.4 %copy-start.2 = (f32[2,409600]{1,0:T(2,128)S(1)}, f32[2,409600]{1,0:T(2,128)}, u32[]{:S(2)}) copy-start(f32[2,409600]{1,0:T(2,128)} %param.25) | copy-start | bytes 9830404
  0.7 262.4 %copy-start.3 = (f32[2,409600]{1,0:T(2,128)S(1)}, f32[2,409600]{1,0:T(2,128)}, u32[]{:S(2)}) copy-start(f32[2,409600]{1,0:T(2,128)} %param.29) | copy-start | bytes 9830404
  0.7 262.4 %copy-start.4 = (f32[4,102400]{1,0:T(4,128)S(1)}, f32[4,102400]{1,0:T(4,128)}, u32[]{:S(2)}) copy-start(f32[4,102400]{1,0:T(4,128)} %param.24) | copy-start | bytes 4915204
  0.7 262.4 %copy-start.5 = (f32[4,102400]{1,0:T(4,128)S(1)}, f32[4,102400]{1,0:T(4,128)}, u32[]{:S(2)}) copy-start(f32[4,102400]{1,0:T(4,128)} %param.28) | copy-start | bytes 4915204
  0.7 262.4 %copy-start.6 = (f32[11,80]{1,0:T(8,128)S(1)}, f32[11,80]{1,0:T(8,128)}, u32[]{:S(2)}) copy-start(f32[11,80]{1,0:T(8,128)} %weight_vec.1) | copy-start | bytes 10564
  0.7 262.4 %copy-start.7 = (f32[11,80]{1,0:T(8,128)S(1)}, f32[11,80]{1,0:T(8,128)}, u32[]{:S(2)}) copy-start(f32[11,80]{1,0:T(8,128)} %first_vec.1) | copy-start | bytes 10564
  0.7 262.4 %copy-start.8 = (f32[11,80]{1,0:T(8,128)S(1)}, f32[11,80]{1,0:T(8,128)}, u32[]{:S(2)}) copy-start(f32[11,80]{1,0:T(8,128)} %second_vec.1) | copy-start | bytes 10564
  0.7 262.4 %copy-start.9 = (f32[1,320]{1,0:T(1,128)S(1)}, f32[1,320]{1,0:T(1,128)}, u32[]{:S(2)}) copy-start(f32[1,320]{1,0:T(1,128)} %weight_wide.1) | copy-start | bytes 3844
  0.8 262.4 %copy-start.10 = (f32[1,320]{1,0:T(1,128)S(1)}, f32[1,320]{1,0:T(1,128)}, u32[]{:S(2)}) copy-start(f32[1,320]{1,0:T(1,128)} %first_wide.1) | copy-start | bytes 3844
  0.8 262.4 %copy-start.11 = (f32[1,320]{1,0:T(1,128)S(1)}, f32[1,320]{1,0:T(1,128)}, u32[]{:S(2)}) copy-start(f32[1,320]{1,0:T(1,128)} %second_wide.1) | copy-start | bytes 3844

commit v5 on v4

--- a/solution.py
+++ b/solution.py
@@ -32,24 +32,25 @@
 MLP_ROWS = 6400
 ROWS = ATTN_ROWS + MLP_ROWS
 THIRD = 3200
-PIECE = 320
+PIECE = 400
 PIECES = THIRD // PIECE
 LOAD_SLOTS = 3
 SEND_SLOTS = 4
 SMALL_ROWS = 16
-BLOCK = 320
+BLOCK = 640
 PARTS = 4
 LAST = THIRD // PARTS
 OWN_PARTS = ((0, 640), (640, 2560))
 CHUNK = 640
 CHUNKS = THIRD // CHUNK
 OUT_SLOTS = 4
-SCATTER_VMEM = 30 * MIB
+SCATTER_VMEM = 36 * MIB
 UPDATE_VMEM = 8 * MIB
 GATHER_VMEM = 2 * MIB
 FINISH_VMEM = 3 * MIB
 CORE = 1
 ORDERS = ((2, 4, 8), (4, 8, 2), (8, 2, 4))
+MASKS = sorted(range(1, GROUP), key=lambda mask: (-(mask // 2).bit_count(), mask))
 UNITS = (
     (0, (0, 1, 2), ()),
     (0, (0, 1), ()),
@@ -75,14 +76,13 @@
     return index
 
 
+def across(me, mask):
+    return flip_all(me, [width for width in (CORE,) + ORDERS[0] if mask & width])
+
+
 def greet_everyone(me):
-    barrier = pltpu.get_barrier_semaphore()
-
-    def signal(step, carry):
-        pl.semaphore_signal(barrier, inc=1, device_id=((me + step) % GROUP,), device_id_type=MESH)
-        return carry
-
-    lax.fori_loop(1, GROUP, signal, 0)
+    for mask in MASKS:
+        pl.semaphore_signal(pltpu.get_barrier_semaphore(), inc=1, device_id=(across(me, mask),), device_id_type=MESH)
 
 
 def meet_everyone():
@@ -90,25 +90,17 @@
 
 
 def tile_to_everyone(me, source_of, slots, send_sems, recv_sems, begin):
-    def copy(step):
-        return pltpu.make_async_remote_copy(
-            source_of((me + step) % GROUP), slots.at[me], send_sems.at[step], recv_sems.at[step],
-            device_id=((me + step) % GROUP,), device_id_type=MESH)
-
-    def arrival(step):
-        return pltpu.make_async_remote_copy(
-            source_of((me + step) % GROUP), slots.at[(me - step + GROUP) % GROUP], send_sems.at[step], recv_sems.at[step],
-            device_id=((me + step) % GROUP,), device_id_type=MESH)
-
-    def start(step, carry):
-        copy(step).start()
-        return carry
-
-    def finish(step, carry):
-        arrival(step).wait()
-        return carry
-
-    lax.fori_loop(1, GROUP, start if begin else finish, 0)
+    for mask in MASKS:
+        other = across(me, mask)
+
+        def copy(slot):
+            return pltpu.make_async_remote_copy(
+                source_of(other), slots.at[slot], send_sems.at[mask], recv_sems.at[mask], device_id=(other,), device_id_type=MESH)
+
+        if begin:
+            copy(me).start()
+        else:
+            copy(other).wait()
 
 
 def small_places(packed, wide, vec):

time: 419 us -> 418 us (level)
  no operation moved by 1% of the time
where the time goes in v5:
time: 418 us
  Pallas kernels  417 us (100%)
    pallas_call x1, Pallas kernels, reduce_scatter(): pl.pallas_call(scatter_kernel, name='scatter', out_shape=(pltpu.VMEM((ROW...  262 us
    pallas_call x1, Pallas kernels, all_gather(): pl.pallas_call(gather_kernel, name='gather', out_shape=(pltpu.VMEM((GROUP...  135 us
    pallas_call x1, Pallas kernels, write_replica(): pl.pallas_call(write_kernel, name='write', out_shape=(pltpu.HBM((GROUP *...  12.9 us

profile of v5, /device:TPU:0, one launch (start us, length us, event | category | flops | bytes accessed | tf_op | source)
XLA Modules:
  0.0 418.1 jit_solution(16612268521938757371)
XLA Ops:
  0.7 0.0 copy-start
  0.7 0.0 copy-start.1
  0.7 0.0 copy-start.2
  0.7 0.0 copy-start.3
  0.7 0.0 copy-start.4
  0.7 0.0 copy-start.5
  0.7 0.0 copy-start.6
  0.7 0.0 copy-start.7
  0.7 0.0 copy-start.8
  0.7 0.0 copy-start.9
  0.8 0.0 copy-start.10
  0.8 0.0 copy-start.11
  0.8 262.0 %scatter.1 = (f32[9600,128]{1,0:T(8,128)S(1)}, f32[16,128]{1,0:T(8,128)S(1)}, f32[8,128]{1,0:T(8,128)S(1)}, bf16[7,3,3200,128]{3,2,1,0:T(8,128)(2,1)}, f32[6,3,3200,128]{3,2,1,0:T(8,128)}) custom-call(bf16[16,3200,128]{2,1,0:T(8,128)(2,1)} %bitcast.91, bf16[16,6400,128]{2,1,0:T(8,128)(2,1)} %bitcast.90, bf16[1,5120]{1,0:T(2,128)(2,1)} %bitcast.93, ...), custom_call_target="tpu_custom_call" | custom-call | tf_op jit(solution)/shard_map/scatter/pallas_call | solution.py:341
  262.8 0.0 copy-done
  262.8 0.0 copy-done.1
  262.8 0.0 copy-done.2
  262.8 0.0 copy-done.3
  262.8 0.0 copy-done.4
  262.9 0.0 copy-done.5
  262.9 0.0 copy-done.6
  262.9 0.0 copy-done.7
  262.9 0.0 copy-done.8
  262.9 0.0 copy-done.9
  262.9 0.0 copy-done.10
  262.9 0.0 copy-done.11
  262.9 5.2 %update.1 = (f32[9600,128]{1,0:T(8,128)S(1)}, f32[16,128]{1,0:T(8,128)S(1)}, f32[16,128]{1,0:T(8,128)S(1)}, f32[8,128]{1,0:T(8,128)S(1)}, f32[3200,128]{1,0:T(8,...) custom-call(f32[9600,128]{1,0:T(8,128)S(1)} %get-tuple-element.47.su, ...), custom_call_target="tpu_custom_call" | custom-call | tf_op jit(solution)/shard_map/update/pallas_call | solution.py:492
  268.1 134.8 %gather.1 = (bf16[16,9600,128]{2,1,0:T(8,128)(2,1)S(1)}, bf16[1,5120]{1,0:T(2,128)(2,1)S(1)}, bf16[11,1280]{1,0:T(8,128)(2,1)S(1)}, f32[9600,128]{1,0:T(8,128)S(...) custom-call(f32[8,128]{1,0:T(8,128)S(1)} %get-tuple-element.50.part_sums, f32[3200,128]{1,0:T(8,128)S(1)} %bitcast.85, ...), custom_call_target="tpu_custom_call" | custom-call | tf_op jit(solution)/shard_map/gather/pallas_call | solution.py:688
  402.9 12.9 %write.1 = (bf16[51200,128]{1,0:T(8,128)(2,1)}, bf16[102400,128]{1,0:T(8,128)(2,1)}) custom-call(bf16[16,9600,128]{2,1,0:T(8,128)(2,1)S(1)} %get-tuple-element.54.everything), custom_call_target="tpu_custom_call" | custom-call | tf_op jit(solution)/shard_map/write/pallas_call | solution.py:731
  415.8 2.3 finish.1
Async XLA Ops:
  0.7 262.2 %copy-start = (f32[2,409600]{1,0:T(2,128)S(1)}, f32[2,409600]{1,0:T(2,128)}, u32[]{:S(2)}) copy-start(f32[2,409600]{1,0:T(2,128)} %param.21) | copy-start | bytes 9830404
  0.7 262.2 %copy-start.1 = (f32[4,102400]{1,0:T(4,128)S(1)}, f32[4,102400]{1,0:T(4,128)}, u32[]{:S(2)}) copy-start(f32[4,102400]{1,0:T(4,128)} %param.20) | copy-start | bytes 4915204
  0.7 262.2 %copy-start.2 = (f32[2,409600]{1,0:T(2,128)S(1)}, f32[2,409600]{1,0:T(2,128)}, u32[]{:S(2)}) copy-start(f32[2,409600]{1,0:T(2,128)} %param.25) | copy-start | bytes 9830404
  0.7 262.2 %copy-start.3 = (f32[2,409600]{1,0:T(2,128)S(1)}, f32[2,409600]{1,0:T(2,128)}, u32[]{:S(2)}) copy-start(f32[2,409600]{1,0:T(2,128)} %param.29) | copy-start | bytes 9830404
  0.7 262.2 %copy-start.4 = (f32[4,102400]{1,0:T(4,128)S(1)}, f32[4,102400]{1,0:T(4,128)}, u32[]{:S(2)}) copy-start(f32[4,102400]{1,0:T(4,128)} %param.24) | copy-start | bytes 4915204
  0.7 262.2 %copy-start.5 = (f32[4,102400]{1,0:T(4,128)S(1)}, f32[4,102400]{1,0:T(4,128)}, u32[]{:S(2)}) copy-start(f32[4,102400]{1,0:T(4,128)} %param.28) | copy-start | bytes 4915204
  0.7 262.2 %copy-start.6 = (f32[11,80]{1,0:T(8,128)S(1)}, f32[11,80]{1,0:T(8,128)}, u32[]{:S(2)}) copy-start(f32[11,80]{1,0:T(8,128)} %weight_vec.1) | copy-start | bytes 10564
  0.7 262.2 %copy-start.7 = (f32[11,80]{1,0:T(8,128)S(1)}, f32[11,80]{1,0:T(8,128)}, u32[]{:S(2)}) copy-start(f32[11,80]{1,0:T(8,128)} %first_vec.1) | copy-start | bytes 10564
  0.7 262.2 %copy-start.8 = (f32[11,80]{1,0:T(8,128)S(1)}, f32[11,80]{1,0:T(8,128)}, u32[]{:S(2)}) copy-start(f32[11,80]{1,0:T(8,128)} %second_vec.1) | copy-start | bytes 10564
  0.7 262.2 %copy-start.9 = (f32[1,320]{1,0:T(1,128)S(1)}, f32[1,320]{1,0:T(1,128)}, u32[]{:S(2)}) copy-start(f32[1,320]{1,0:T(1,128)} %weight_wide.1) | copy-start | bytes 3844
  0.8 262.2 %copy-start.10 = (f32[1,320]{1,0:T(1,128)S(1)}, f32[1,320]{1,0:T(1,128)}, u32[]{:S(2)}) copy-start(f32[1,320]{1,0:T(1,128)} %first_wide.1) | copy-start | bytes 3844
  0.8 262.2 %copy-start.11 = (f32[1,320]{1,0:T(1,128)S(1)}, f32[1,320]{1,0:T(1,128)}, u32[]{:S(2)}) copy-start(f32[1,320]{1,0:T(1,128)} %second_wide.1) | copy-start | bytes 3844

commit v6 on v5

--- a/solution.py
+++ b/solution.py
@@ -51,6 +51,7 @@
 CORE = 1
 ORDERS = ((2, 4, 8), (4, 8, 2), (8, 2, 4))
 MASKS = sorted(range(1, GROUP), key=lambda mask: (-(mask // 2).bit_count(), mask))
+NEIGHBOURS = (8, 4, 2, 1)
 UNITS = (
     (0, (0, 1, 2), ()),
     (0, (0, 1), ()),
@@ -80,13 +81,13 @@
     return flip_all(me, [width for width in (CORE,) + ORDERS[0] if mask & width])
 
 
-def greet_everyone(me):
-    for mask in MASKS:
+def greet(me, masks):
+    for mask in masks:
         pl.semaphore_signal(pltpu.get_barrier_semaphore(), inc=1, device_id=(across(me, mask),), device_id_type=MESH)
 
 
-def meet_everyone():
-    pl.semaphore_wait(pltpu.get_barrier_semaphore(), GROUP - 1)
+def meet(masks):
+    pl.semaphore_wait(pltpu.get_barrier_semaphore(), len(masks))
 
 
 def tile_to_everyone(me, source_of, slots, send_sems, recv_sems, begin):
@@ -182,7 +183,7 @@
                    small_send, small_recv, square_send, square_recv, local_sems):
     me = lax.axis_index("data")
     twin = flip(me, CORE)
-    greet_everyone(me)
+    greet(me, NEIGHBOURS)
 
     def grad_of(third, owner, row, count):
         if third == 0:
@@ -250,7 +251,7 @@
     ahead = LOAD_SLOTS - 1
     for piece in range(ahead):
         begin(0, piece)
-    meet_everyone()
+    meet(NEIGHBOURS)
     lax.fori_loop(0, PIECES, start_first, 0)
 
     for unit in range(8):
@@ -292,6 +293,10 @@
                     value = value * (1.0 / GROUP)
                     sums[pl.ds(pl.multiple_of(third * THIRD + piece * PIECE, PIECE), PIECE)] = value
                     square_sum[...] += jnp.sum((value * value).reshape(PIECE // 8, 8, LANES), axis=0)
+            if unit == 7:
+                @pl.when(piece == 0)
+                def _():
+                    tile_to_everyone(me, lambda owner: small_shares.at[owner], small_slots, small_send, small_recv, True)
             if unit == 0:
                 @pl.when(piece == 0)
                 def _():
@@ -307,14 +312,12 @@
             shares_from(wide_raw, vec_raw, wide_rows, vec_rows, packed)
             small_shares[...] = packed[...].astype(jnp.bfloat16)
             small_slots[me] = small_shares[me]
-        if unit == 1:
-            tile_to_everyone(me, lambda owner: small_shares.at[owner], small_slots, small_send, small_recv, True)
-        if unit == 5:
-            tile_to_everyone(me, lambda owner: small_shares.at[owner], small_slots, small_send, small_recv, False)
-            small = jnp.sum(small_slots[...].astype(jnp.float32), axis=0) * (1.0 / GROUP)
-            small_sums[...] = small
-            square_sum[...] = (small * small)[0:8] + (small * small)[8:16]
-
+            square_sum[...] = jnp.zeros_like(square_sum)
+
+    tile_to_everyone(me, lambda owner: small_shares.at[owner], small_slots, small_send, small_recv, False)
+    small = jnp.sum(small_slots[...].astype(jnp.float32), axis=0) * (1.0 / GROUP)
+    small_sums[...] = small
+    square_sum[...] += (small * small)[0:8] + (small * small)[8:16]
     square_slots[me] = square_sum[...]
     tile_to_everyone(me, lambda owner: square_sum, square_slots, square_send, square_recv, True)
     for slot in range(SEND_SLOTS):
@@ -519,8 +522,8 @@
                   own_send, own_recv, last_send, last_recv, last_twin_send, last_twin_recv):
     me = lax.axis_index("data")
     twin = flip(me, CORE)
-    greet_everyone(me)
-    meet_everyone()
+    greet(me, MASKS)
+    meet(MASKS)
     slots[me] = part_sums[...]
     tile_to_everyone(me, lambda owner: part_sums, slots, tile_send, tile_recv, True)
     tile_to_everyone(me, lambda owner: part_sums, slots, tile_send, tile_recv, False)

time: 418 us -> 418 us (level)
  no operation moved by 1% of the time
where the time goes in v6:
time: 418 us
  Pallas kernels  417 us (100%)
    pallas_call x1, Pallas kernels, reduce_scatter(): pl.pallas_call(scatter_kernel, name='scatter', out_shape=(pltpu.VMEM((ROW...  261 us
    pallas_call x1, Pallas kernels, all_gather(): pl.pallas_call(gather_kernel, name='gather', out_shape=(pltpu.VMEM((GROUP...  135 us
    pallas_call x1, Pallas kernels, write_replica(): pl.pallas_call(write_kernel, name='write', out_shape=(pltpu.HBM((GROUP *...  12.9 us

profile of v6, /device:TPU:0, one launch (start us, length us, event | category | flops | bytes accessed | tf_op | source)
XLA Modules:
  0.0 417.6 jit_solution(4916743173140131980)
XLA Ops:
  0.7 0.0 copy-start
  0.7 0.0 copy-start.1
  0.7 0.0 copy-start.2
  0.7 0.0 copy-start.3
  0.7 0.0 copy-start.4
  0.7 0.0 copy-start.5
  0.7 0.0 copy-start.6
  0.7 0.0 copy-start.7
  0.7 0.0 copy-start.8
  0.7 0.0 copy-start.9
  0.8 0.0 copy-start.10
  0.8 0.0 copy-start.11
  0.8 261.2 %scatter.1 = (f32[9600,128]{1,0:T(8,128)S(1)}, f32[16,128]{1,0:T(8,128)S(1)}, f32[8,128]{1,0:T(8,128)S(1)}, bf16[7,3,3200,128]{3,2,1,0:T(8,128)(2,1)}, f32[6,3,3200,128]{3,2,1,0:T(8,128)}) custom-call(bf16[16,3200,128]{2,1,0:T(8,128)(2,1)} %bitcast.91, bf16[16,6400,128]{2,1,0:T(8,128)(2,1)} %bitcast.90, bf16[1,5120]{1,0:T(2,128)(2,1)} %bitcast.93, ...), custom_call_target="tpu_custom_call" | custom-call | tf_op jit(solution)/shard_map/scatter/pallas_call | solution.py:344
  262.0 0.0 copy-done
  262.0 0.0 copy-done.1
  262.0 0.0 copy-done.2
  262.0 0.0 copy-done.3
  262.1 0.0 copy-done.4
  262.1 0.0 copy-done.5
  262.1 0.0 copy-done.6
  262.1 0.0 copy-done.7
  262.1 0.0 copy-done.8
  262.1 0.0 copy-done.9
  262.1 0.0 copy-done.10
  262.1 0.0 copy-done.11
  262.1 5.2 %update.1 = (f32[9600,128]{1,0:T(8,128)S(1)}, f32[16,128]{1,0:T(8,128)S(1)}, f32[16,128]{1,0:T(8,128)S(1)}, f32[8,128]{1,0:T(8,128)S(1)}, f32[3200,128]{1,0:T(8,...) custom-call(f32[9600,128]{1,0:T(8,128)S(1)} %get-tuple-element.47.su, ...), custom_call_target="tpu_custom_call" | custom-call | tf_op jit(solution)/shard_map/update/pallas_call | solution.py:495
  267.3 135.0 %gather.1 = (bf16[16,9600,128]{2,1,0:T(8,128)(2,1)S(1)}, bf16[1,5120]{1,0:T(2,128)(2,1)S(1)}, bf16[11,1280]{1,0:T(8,128)(2,1)S(1)}, f32[9600,128]{1,0:T(8,128)S(...) custom-call(f32[8,128]{1,0:T(8,128)S(1)} %get-tuple-element.50.part_sums, f32[3200,128]{1,0:T(8,128)S(1)} %bitcast.85, ...), custom_call_target="tpu_custom_call" | custom-call | tf_op jit(solution)/shard_map/gather/pallas_call | solution.py:691
  402.3 12.9 %write.1 = (bf16[51200,128]{1,0:T(8,128)(2,1)}, bf16[102400,128]{1,0:T(8,128)(2,1)}) custom-call(bf16[16,9600,128]{2,1,0:T(8,128)(2,1)S(1)} %get-tuple-element.54.everything), custom_call_target="tpu_custom_call" | custom-call | tf_op jit(solution)/shard_map/write/pallas_call | solution.py:734
  415.2 2.3 finish.1
Async XLA Ops:
  0.7 261.4 %copy-start = (f32[2,409600]{1,0:T(2,128)S(1)}, f32[2,409600]{1,0:T(2,128)}, u32[]{:S(2)}) copy-start(f32[2,409600]{1,0:T(2,128)} %param.21) | copy-start | bytes 9830404
  0.7 261.4 %copy-start.1 = (f32[4,102400]{1,0:T(4,128)S(1)}, f32[4,102400]{1,0:T(4,128)}, u32[]{:S(2)}) copy-start(f32[4,102400]{1,0:T(4,128)} %param.20) | copy-start | bytes 4915204
  0.7 261.4 %copy-start.2 = (f32[2,409600]{1,0:T(2,128)S(1)}, f32[2,409600]{1,0:T(2,128)}, u32[]{:S(2)}) copy-start(f32[2,409600]{1,0:T(2,128)} %param.25) | copy-start | bytes 9830404
  0.7 261.4 %copy-start.3 = (f32[2,409600]{1,0:T(2,128)S(1)}, f32[2,409600]{1,0:T(2,128)}, u32[]{:S(2)}) copy-start(f32[2,409600]{1,0:T(2,128)} %param.29) | copy-start | bytes 9830404
  0.7 261.4 %copy-start.4 = (f32[4,102400]{1,0:T(4,128)S(1)}, f32[4,102400]{1,0:T(4,128)}, u32[]{:S(2)}) copy-start(f32[4,102400]{1,0:T(4,128)} %param.24) | copy-start | bytes 4915204
  0.7 261.4 %copy-start.5 = (f32[4,102400]{1,0:T(4,128)S(1)}, f32[4,102400]{1,0:T(4,128)}, u32[]{:S(2)}) copy-start(f32[4,102400]{1,0:T(4,128)} %param.28) | copy-start | bytes 4915204
  0.7 261.4 %copy-start.6 = (f32[11,80]{1,0:T(8,128)S(1)}, f32[11,80]{1,0:T(8,128)}, u32[]{:S(2)}) copy-start(f32[11,80]{1,0:T(8,128)} %weight_vec.1) | copy-start | bytes 10564
  0.7 261.4 %copy-start.7 = (f32[11,80]{1,0:T(8,128)S(1)}, f32[11,80]{1,0:T(8,128)}, u32[]{:S(2)}) copy-start(f32[11,80]{1,0:T(8,128)} %first_vec.1) | copy-start | bytes 10564
  0.7 261.4 %copy-start.8 = (f32[11,80]{1,0:T(8,128)S(1)}, f32[11,80]{1,0:T(8,128)}, u32[]{:S(2)}) copy-start(f32[11,80]{1,0:T(8,128)} %second_vec.1) | copy-start | bytes 10564
  0.7 261.4 %copy-start.9 = (f32[1,320]{1,0:T(1,128)S(1)}, f32[1,320]{1,0:T(1,128)}, u32[]{:S(2)}) copy-start(f32[1,320]{1,0:T(1,128)} %weight_wide.1) | copy-start | bytes 3844
  0.8 261.4 %copy-start.10 = (f32[1,320]{1,0:T(1,128)S(1)}, f32[1,320]{1,0:T(1,128)}, u32[]{:S(2)}) copy-start(f32[1,320]{1,0:T(1,128)} %first_wide.1) | copy-start | bytes 3844
  0.8 261.4 %copy-start.11 = (f32[1,320]{1,0:T(1,128)S(1)}, f32[1,320]{1,0:T(1,128)}, u32[]{:S(2)}) copy-start(f32[1,320]{1,0:T(1,128)} %second_wide.1) | copy-start | bytes 3844

commit v7 on v6

--- a/solution.py
+++ b/solution.py
@@ -40,7 +40,8 @@
 BLOCK = 640
 PARTS = 4
 LAST = THIRD // PARTS
-OWN_PARTS = ((0, 640), (640, 2560))
+OWN_PARTS = ((0, 320), (320, 960), (1280, 1920))
+REFRESH = 320
 CHUNK = 640
 CHUNKS = THIRD // CHUNK
 OUT_SLOTS = 4
@@ -603,15 +604,15 @@
             weight, base = bank_part(third, weight_attn, weight_mlp)
 
             def refresh(piece, carry, third=third, scale=scale, weight=weight, base=base, first_row=first_row):
-                row = first_row + piece * BLOCK
-                rows = pl.ds(pl.multiple_of(third * THIRD + row, BLOCK), BLOCK)
-                old = weight[pl.ds(pl.multiple_of(base + row, BLOCK), BLOCK)].reshape((-1,) + TILE)
-                new = (old - scale[None] * update[rows].reshape((-1,) + TILE)).reshape(BLOCK, LANES)
+                row = first_row + piece * REFRESH
+                rows = pl.ds(pl.multiple_of(third * THIRD + row, REFRESH), REFRESH)
+                old = weight[pl.ds(pl.multiple_of(base + row, REFRESH), REFRESH)].reshape((-1,) + TILE)
+                new = (old - scale[None] * update[rows].reshape((-1,) + TILE)).reshape(REFRESH, LANES)
                 new_weight[rows] = new
                 everything[me, rows] = new.astype(jnp.bfloat16)
                 return carry
 
-            lax.fori_loop(0, rows_here // BLOCK, refresh, 0)
+            lax.fori_loop(0, rows_here // REFRESH, refresh, 0)
             own_part(third, part, me).start()
     for stage in (1, 2):
         for third in THIRDS:

time: 418 us -> 418 us (level)
  no operation moved by 1% of the time
where the time goes in v7:
time: 418 us; the launch traced here: 417 us
  Pallas kernels  417 us (100%)
    pallas_call x1, Pallas kernels, reduce_scatter(): pl.pallas_call(scatter_kernel, name='scatter', out_shape=(pltpu.VMEM((ROW...  261 us
    pallas_call x1, Pallas kernels, all_gather(): pl.pallas_call(gather_kernel, name='gather', out_shape=(pltpu.VMEM((GROUP...  135 us
    pallas_call x1, Pallas kernels, write_replica(): pl.pallas_call(write_kernel, name='write', out_shape=(pltpu.HBM((GROUP *...  12.9 us

profile of v7, /device:TPU:0, one launch (start us, length us, event | category | flops | bytes accessed | tf_op | source)
XLA Modules:
  0.0 417.5 jit_solution(18077440442111568924)
XLA Ops:
  0.7 0.0 copy-start
  0.7 0.0 copy-start.1
  0.7 0.0 copy-start.2
  0.7 0.0 copy-start.3
  0.7 0.0 copy-start.4
  0.7 0.0 copy-start.5
  0.7 0.0 copy-start.6
  0.7 0.0 copy-start.7
  0.7 0.0 copy-start.8
  0.7 0.0 copy-start.9
  0.8 0.0 copy-start.10
  0.8 0.0 copy-start.11
  0.8 261.2 %scatter.1 = (f32[9600,128]{1,0:T(8,128)S(1)}, f32[16,128]{1,0:T(8,128)S(1)}, f32[8,128]{1,0:T(8,128)S(1)}, bf16[7,3,3200,128]{3,2,1,0:T(8,128)(2,1)}, f32[6,3,3200,128]{3,2,1,0:T(8,128)}) custom-call(bf16[16,3200,128]{2,1,0:T(8,128)(2,1)} %bitcast.91, bf16[16,6400,128]{2,1,0:T(8,128)(2,1)} %bitcast.90, bf16[1,5120]{1,0:T(2,128)(2,1)} %bitcast.93, ...), custom_call_target="tpu_custom_call" | custom-call | tf_op jit(solution)/shard_map/scatter/pallas_call | solution.py:345
  262.0 0.0 copy-done
  262.0 0.0 copy-done.1
  262.0 0.0 copy-done.2
  262.0 0.0 copy-done.3
  262.1 0.0 copy-done.4
  262.1 0.0 copy-done.5
  262.1 0.0 copy-done.6
  262.1 0.0 copy-done.7
  262.1 0.0 copy-done.8
  262.1 0.0 copy-done.9
  262.1 0.0 copy-done.10
  262.1 0.0 copy-done.11
  262.1 5.2 %update.1 = (f32[9600,128]{1,0:T(8,128)S(1)}, f32[16,128]{1,0:T(8,128)S(1)}, f32[16,128]{1,0:T(8,128)S(1)}, f32[8,128]{1,0:T(8,128)S(1)}, f32[3200,128]{1,0:T(8,...) custom-call(f32[9600,128]{1,0:T(8,128)S(1)} %get-tuple-element.47.su, ...), custom_call_target="tpu_custom_call" | custom-call | tf_op jit(solution)/shard_map/update/pallas_call | solution.py:496
  267.3 134.9 %gather.1 = (bf16[16,9600,128]{2,1,0:T(8,128)(2,1)S(1)}, bf16[1,5120]{1,0:T(2,128)(2,1)S(1)}, bf16[11,1280]{1,0:T(8,128)(2,1)S(1)}, f32[9600,128]{1,0:T(8,128)S(...) custom-call(f32[8,128]{1,0:T(8,128)S(1)} %get-tuple-element.50.part_sums, f32[3200,128]{1,0:T(8,128)S(1)} %bitcast.85, ...), custom_call_target="tpu_custom_call" | custom-call | tf_op jit(solution)/shard_map/gather/pallas_call | solution.py:692
  402.2 12.9 %write.1 = (bf16[51200,128]{1,0:T(8,128)(2,1)}, bf16[102400,128]{1,0:T(8,128)(2,1)}) custom-call(bf16[16,9600,128]{2,1,0:T(8,128)(2,1)S(1)} %get-tuple-element.54.everything), custom_call_target="tpu_custom_call" | custom-call | tf_op jit(solution)/shard_map/write/pallas_call | solution.py:735
  415.2 2.3 finish.1
Async XLA Ops:
  0.7 261.4 %copy-start = (f32[2,409600]{1,0:T(2,128)S(1)}, f32[2,409600]{1,0:T(2,128)}, u32[]{:S(2)}) copy-start(f32[2,409600]{1,0:T(2,128)} %param.21) | copy-start | bytes 9830404
  0.7 261.4 %copy-start.1 = (f32[4,102400]{1,0:T(4,128)S(1)}, f32[4,102400]{1,0:T(4,128)}, u32[]{:S(2)}) copy-start(f32[4,102400]{1,0:T(4,128)} %param.20) | copy-start | bytes 4915204
  0.7 261.4 %copy-start.2 = (f32[2,409600]{1,0:T(2,128)S(1)}, f32[2,409600]{1,0:T(2,128)}, u32[]{:S(2)}) copy-start(f32[2,409600]{1,0:T(2,128)} %param.25) | copy-start | bytes 9830404
  0.7 261.4 %copy-start.3 = (f32[2,409600]{1,0:T(2,128)S(1)}, f32[2,409600]{1,0:T(2,128)}, u32[]{:S(2)}) copy-start(f32[2,409600]{1,0:T(2,128)} %param.29) | copy-start | bytes 9830404
  0.7 261.4 %copy-start.4 = (f32[4,102400]{1,0:T(4,128)S(1)}, f32[4,102400]{1,0:T(4,128)}, u32[]{:S(2)}) copy-start(f32[4,102400]{1,0:T(4,128)} %param.24) | copy-start | bytes 4915204
  0.7 261.4 %copy-start.5 = (f32[4,102400]{1,0:T(4,128)S(1)}, f32[4,102400]{1,0:T(4,128)}, u32[]{:S(2)}) copy-start(f32[4,102400]{1,0:T(4,128)} %param.28) | copy-start | bytes 4915204
  0.7 261.4 %copy-start.6 = (f32[11,80]{1,0:T(8,128)S(1)}, f32[11,80]{1,0:T(8,128)}, u32[]{:S(2)}) copy-start(f32[11,80]{1,0:T(8,128)} %weight_vec.1) | copy-start | bytes 10564
  0.7 261.4 %copy-start.7 = (f32[11,80]{1,0:T(8,128)S(1)}, f32[11,80]{1,0:T(8,128)}, u32[]{:S(2)}) copy-start(f32[11,80]{1,0:T(8,128)} %first_vec.1) | copy-start | bytes 10564
  0.7 261.4 %copy-start.8 = (f32[11,80]{1,0:T(8,128)S(1)}, f32[11,80]{1,0:T(8,128)}, u32[]{:S(2)}) copy-start(f32[11,80]{1,0:T(8,128)} %second_vec.1) | copy-start | bytes 10564
  0.7 261.4 %copy-start.9 = (f32[1,320]{1,0:T(1,128)S(1)}, f32[1,320]{1,0:T(1,128)}, u32[]{:S(2)}) copy-start(f32[1,320]{1,0:T(1,128)} %weight_wide.1) | copy-start | bytes 3844
  0.8 261.4 %copy-start.10 = (f32[1,320]{1,0:T(1,128)S(1)}, f32[1,320]{1,0:T(1,128)}, u32[]{:S(2)}) copy-start(f32[1,320]{1,0:T(1,128)} %first_wide.1) | copy-start | bytes 3844
  0.8 261.4 %copy-start.11 = (f32[1,320]{1,0:T(1,128)S(1)}, f32[1,320]{1,0:T(1,128)}, u32[]{:S(2)}) copy-start(f32[1,320]{1,0:T(1,128)} %second_wide.1) | copy-start | bytes 3844
